TPU v7x, 128 devices: a whole 4x4x4 slice. The times are simulated.
128 devices in a mesh: data: 1, dap: 128 (over z, y, x, core).
Axes of the slice: x: 4, y: 4, z: 4, core: 2. Of those that a mesh axis runs over, the one named last changes fastest.
Arguments:
- z: bfloat16 [1536, 1536, 128], P(('data', 'dap'))
- mask: int32 [1536, 1536], P(('data', 'dap'))
- ln_scale: bfloat16 [128], replicated
- ln_bias: bfloat16 [128], replicated
- w_a: bfloat16 [128, 128], replicated
- w_a_gate: bfloat16 [128, 128], replicated
- w_b: bfloat16 [128, 128], replicated
- w_b_gate: bfloat16 [128, 128], replicated
- w_gate: bfloat16 [128, 128], replicated
- ln_hid_scale: bfloat16 [128], replicated
- ln_hid_bias: bfloat16 [128], replicated
- w_out: bfloat16 [128, 128], replicated
Outputs:
- output: bfloat16 [1536, 1536, 128], P(('data', 'dap'))
All inputs are finite; a program needn't handle non-finite values.
Results may differ from a plain program's by a relative error of at most 0.00375147.
Values are sent between devices in bfloat16 or wider.
A program may use at most 1 GiB of HBM per device.

v0:
```python
import jax
import jax.numpy as jnp
from jax import lax
from jax.sharding import PartitionSpec as P, NamedSharding

LN_EPS = 1e-5


def layer_norm(vals, scale, bias, axis):
    mean_val = jnp.mean(vals, axis=axis, keepdims=True)
    centered = vals - mean_val
    variance = jnp.mean(centered * centered, axis=axis, keepdims=True)
    return centered * lax.rsqrt(variance + LN_EPS) * scale + bias


def gated_pair(x_norm, mask_loc, w_cat):
    hidden = w_cat.shape[1] // 4
    local_rows, crop_len = mask_loc.shape
    projected = jnp.einsum('rkd,de->erk', x_norm, w_cat, preferred_element_type=jnp.float32)
    projected = projected.reshape(4, hidden, local_rows, crop_len)
    mask_f = mask_loc.astype(jnp.float32)[None]
    a_side = (mask_f * jax.nn.sigmoid(projected[1]) * projected[0]).astype(jnp.bfloat16)
    b_side = (mask_f * jax.nn.sigmoid(projected[3]) * projected[2]).astype(jnp.bfloat16)
    return a_side, b_side


def finish_rows(z_loc, x_norm, tri_rows, w_gate, ln_hid_scale, ln_hid_bias, w_out):
    y_norm = layer_norm(tri_rows.astype(jnp.float32), ln_hid_scale[:, None, None], ln_hid_bias[:, None, None], 0).astype(jnp.bfloat16)
    update = jnp.einsum('crk,cd->rkd', y_norm, w_out, preferred_element_type=jnp.float32)
    gate_val = jax.nn.sigmoid(jnp.einsum('rkd,de->rke', x_norm, w_gate, preferred_element_type=jnp.float32))
    return (z_loc.astype(jnp.float32) + gate_val * update).astype(jnp.bfloat16)


def solution(mesh):
    row_spec = P(('data', 'dap'), None, None)
    mask_spec = P(('data', 'dap'), None)
    replicated = P()

    def local_fn(z_loc, mask_loc, ln_scale, ln_bias, w_a, w_a_gate, w_b, w_b_gate, w_gate, ln_hid_scale, ln_hid_bias, w_out):
        x_norm = layer_norm(z_loc.astype(jnp.float32), ln_scale, ln_bias, -1).astype(jnp.bfloat16)
        w_cat = jnp.concatenate([w_a, w_a_gate, w_b, w_b_gate], axis=1)
        a_side, b_side = gated_pair(x_norm, mask_loc, w_cat)
        a_chan = lax.all_to_all(a_side, 'dap', 0, 1, tiled=True)
        b_chan = lax.all_to_all(b_side, 'dap', 0, 1, tiled=True)
        tri_chan = jnp.einsum('cik,cjk->cij', a_chan, b_chan, preferred_element_type=jnp.float32).astype(jnp.bfloat16)
        tri_rows = lax.all_to_all(tri_chan, 'dap', 1, 0, tiled=True)
        return finish_rows(z_loc, x_norm, tri_rows, w_gate, ln_hid_scale, ln_hid_bias, w_out)

    return jax.shard_map(local_fn, mesh=mesh, in_specs=(row_spec, mask_spec) + (replicated,) * 10, out_specs=row_spec, check_vma=False)
```

profile of v0, /device:TPU:1, one launch (start us, length us, event | category | flops | bytes accessed | tf_op | source)
XLA Modules:
  0.0 533.5 jit_solution(669069415216551789)
XLA Ops:
  3.8 7.2 %fusion.2 = f32[12,1536]{1,0:T(8,128)S(1)} fusion(bf16[12,1536,128]{2,1,0:T(8,128)(2,1)} %param.12, f32[12,1536]{1,0:T(8,128)S(1)} %broadcast_multiply_fusion.1), kind=kLoop, calls=%fused_computation.7 | loop fusion | flops 9418752 | bytes 4866048 | tf_op jit(solution)/shard_map/reduce_sum | solution.py:12
  11.6 15.4 %fusion.19 = f32[512,12,1536]{2,0,1:T(8,128)} fusion(bf16[12,1536,128]{2,1,0:T(8,128)(2,1)} %param.12, f32[128]{0:T(128)S(1)} %convert_element_type.56, f32[128]{0:T(128)S(1)} %convert_element_type.55, f32[12,1536]{1,0:T(8,128)S(1)} %add_rsqrt_fusion.1, f32[12,1536]{1,0:T(8,128)S(1)} %broadcast_multiply_fusion.1, bf16[128,128]{0,1:T(8,128)(2,1)S(1)} %copy.28, ...), kind=kOutput, calls=%fused_computation.30 | convolution fusion | flops 2430599168 | bytes 42746880 | tf_op jit(solution)/shard_map/rkd,de->erk/dot_general | solution.py:19
  27.0 16.4 %fusion.7 = (bf16[128,12,1536]{2,0,1:T(8,128)(2,1)}, bf16[128,12,1536]{2,0,1:T(8,128)(2,1)S(1)}) fusion(f32[512,12,1536]{2,0,1:T(8,128)} %fusion.19, f32[12,1536]{1,0:T(8,128)S(1)} %convert_element_type.58), kind=kLoop, calls=%fused_computation.13 | loop fusion | flops 28311552 | bytes 47259648 | tf_op jit(solution)/shard_map/convert_element_type | solution.py:23
  43.4 5.4 %copy.29 = bf16[128,12,1536]{2,1,0:T(8,128)(2,1)} copy(bf16[128,12,1536]{2,0,1:T(8,128)(2,1)S(1)} %get-tuple-element.6) | data formatting | bytes 9437184 | tf_op jit(solution)/shard_map/convert_element_type | solution.py:22
  48.7 12.2 %all-to-all-start = ((bf16[128,12,1536]{2,1,0:T(8,128)(2,1)}), bf16[128,12,1536]{2,1,0:T(8,128)(2,1)}, u32[]{:S(2)}, u32[]{:S(2)}) async-start(bf16[128,12,1536]{2,1,0:T(8,128)(2,1)} %copy.29), calls=%async_computation | async-start | bytes 12582912 | tf_op jit(solution)/shard_map/all_to_all | solution.py:43
  61.0 7.6 %copy.30 = bf16[128,12,1536]{2,1,0:T(8,128)(2,1)} copy(bf16[128,12,1536]{2,0,1:T(8,128)(2,1)} %get-tuple-element.5) | data formatting | bytes 9437184 | tf_op jit(solution)/shard_map/convert_element_type | solution.py:23
  68.6 82.3 %all-to-all-done = bf16[128,12,1536]{2,1,0:T(8,128)(2,1)} async-done(((bf16[128,12,1536]{2,1,0:T(8,128)(2,1)}), bf16[128,12,1536]{2,1,0:T(8,128)(2,1)}, u32[]{:S(2)}, u32[]{:S(2)}) %all-to-all-start) | async-done | bytes 4718624 | tf_op jit(solution)/shard_map/all_to_all | solution.py:43
  150.9 7.1 %all-to-all-start.1 = ((bf16[128,12,1536]{2,1,0:T(8,128)(2,1)}), bf16[128,12,1536]{2,1,0:T(8,128)(2,1)}, u32[]{:S(2)}, u32[]{:S(2)}) async-start(bf16[128,12,1536]{2,1,0:T(8,128)(2,1)} %copy.30), calls=%async_computation.1 | async-start | bytes 12582912 | tf_op jit(solution)/shard_map/all_to_all | solution.py:44
  158.0 8.2 %reshape.64 = bf16[1536,1536]{1,0:T(8,128)(2,1)} reshape(bf16[128,12,1536]{2,1,0:T(8,128)(2,1)} %all-to-all-done) | data formatting | bytes 9437184 | tf_op jit(solution)/shard_map/reshape.13
  166.2 74.1 %all-to-all-done.1 = bf16[128,12,1536]{2,1,0:T(8,128)(2,1)} async-done(((bf16[128,12,1536]{2,1,0:T(8,128)(2,1)}), bf16[128,12,1536]{2,1,0:T(8,128)(2,1)}, u32[]{:S(2)}, u32[]{:S(2)}) %all-to-all-start.1) | async-done | bytes 4718624 | tf_op jit(solution)/shard_map/all_to_all | solution.py:44
  240.3 8.2 %reshape.65 = bf16[1536,1536]{1,0:T(8,128)(2,1)} reshape(bf16[128,12,1536]{2,1,0:T(8,128)(2,1)} %all-to-all-done.1) | data formatting | bytes 9437184 | tf_op jit(solution)/shard_map/reshape.14
  248.5 10.8 %fusion.17 = bf16[1,1536,1536]{2,1,0:T(8,128)(2,1)S(1)} fusion(bf16[1536,1536]{1,0:T(8,128)(2,1)} %reshape.64, bf16[1536,1536]{1,0:T(8,128)(2,1)} %reshape.65), kind=kOutput, calls=%fused_computation.28 | convolution fusion | flops 7250116608 | bytes 14155776 | tf_op jit(solution)/shard_map/cik,cjk->cij/dot_general | solution.py:45
  259.4 52.2 %copy.37 = bf16[1,1536,1536]{2,0,1:T(2,128)(2,1)} copy(bf16[1,1536,1536]{2,1,0:T(8,128)(2,1)S(1)} %fusion.17) | data formatting | bytes 9437184 | tf_op jit(solution)/shard_map/convert_element_type | solution.py:45
  312.1 31.8 %reduce.2 = bf16[1536,1536]{1,0:T(8,128)(2,1)} reduce(bf16[1536,1,1536]{2,1,0:T(2,128)(2,1)} %bitcast.20, bf16[]{:T(256)} %broadcast.66), dimensions={1}, to_apply=%bitcast.17.reduce_sub_computation | reduce | bytes 9437186
  343.9 11.4 %reshape.71 = bf16[128,2,9216]{2,1,0:T(2,128)(2,1)} reshape(bf16[1536,1536]{1,0:T(8,128)(2,1)} %reduce.2) | data formatting | bytes 9437184
  355.3 14.1 %all-to-all-start.2 = ((bf16[128,2,9216]{2,1,0:T(2,128)(2,1)}), bf16[128,2,9216]{2,1,0:T(2,128)(2,1)}, u32[]{:S(2)}, u32[]{:S(2)}) async-start(bf16[128,2,9216]{2,1,0:T(2,128)(2,1)} %reshape.71), calls=%async_computation.2 | async-start | bytes 9437184 | tf_op jit(solution)/shard_map/all_to_all | solution.py:46
  369.5 9.9 %fusion.21 = f32[12,1536,128]{2,1,0:T(8,128)} fusion(bf16[12,1536,128]{2,1,0:T(8,128)(2,1)} %param.12, f32[128]{0:T(128)S(1)} %convert_element_type.56, f32[128]{0:T(128)S(1)} %convert_element_type.55, f32[12,1536]{1,0:T(8,128)S(1)} %add_rsqrt_fusion.1, f32[12,1536]{1,0:T(8,128)S(1)} %broadcast_multiply_fusion.1, bf16[128,128]{1,0:T(8,128)(2,1)S(1)} %copy-done), kind=kOutput, calls=%fused_computation.31 | convolution fusion | flops 618135552 | bytes 14337024 | tf_op jit(solution)/shard_map/rkd,de->rke/dot_general | solution.py:30
  379.4 56.9 %all-to-all-done.2 = bf16[128,2,9216]{2,1,0:T(2,128)(2,1)} async-done(((bf16[128,2,9216]{2,1,0:T(2,128)(2,1)}), bf16[128,2,9216]{2,1,0:T(2,128)(2,1)}, u32[]{:S(2)}, u32[]{:S(2)}) %all-to-all-start.2) | async-done | bytes 4718624 | tf_op jit(solution)/shard_map/all_to_all | solution.py:46
  436.3 19.9 %reshape.72 = bf16[1536,1,1536]{2,1,0:T(2,128)(2,1)} reshape(bf16[128,2,9216]{2,1,0:T(2,128)(2,1)} %all-to-all-done.2) | data formatting | bytes 9437184
  456.2 32.3 %convert_reduce_fusion.1 = f32[1536,1536]{1,0:T(8,128)} fusion(bf16[1536,1,1536]{2,1,0:T(2,128)(2,1)} %reshape.72), kind=kLoop, calls=%fused_computation.26 | loop fusion | flops 2359296 | bytes 14155776 | tf_op jit(solution)/shard_map/convert_element_type | solution.py:28
  488.5 11.3 %reshape.66 = f32[128,12,1536]{2,1,0:T(8,128)} reshape(f32[1536,1536]{1,0:T(8,128)} %convert_reduce_fusion.1) | data formatting | bytes 18874368 | tf_op jit(solution)/shard_map/convert_element_type | solution.py:28
  499.8 5.3 reduce_sum.38
  505.2 6.4 %multiply_reduce_fusion = f32[12,1536]{1,0:T(8,128)S(1)} fusion(f32[128,12,1536]{2,1,0:T(8,128)} %reshape.66, f32[12,1536]{1,0:T(8,128)S(1)} %broadcast_multiply_fusion), kind=kLoop, calls=%fused_computation.4 | loop fusion | flops 7059456 | bytes 9584640 | tf_op jit(solution)/shard_map/reduce_sum | solution.py:12
  518.5 14.5 %fusion.6 = bf16[12,1536,128]{2,1,0:T(8,128)(2,1)} fusion(bf16[12,1536,128]{2,1,0:T(8,128)(2,1)S(1)} %bitcast.19, f32[12,1536,128]{2,1,0:T(8,128)} %fusion.21, bf16[128,12,1536]{2,1,0:T(8,128)(2,1)} %add_convert_fusion, bf16[128,128]{1,0:T(8,128)(2,1)S(1)} %copy-done.7), kind=kOutput, calls=%fused_computation.11 | convolution fusion | flops 620494848 | bytes 23625728 | tf_op jit(solution)/shard_map/crk,cd->rkd/dot_general | solution.py:29
  (45 shorter events, 11.7 us)
Async XLA Ops:
  0.0 369.5 %copy-start = (bf16[128,128]{1,0:T(8,128)(2,1)S(1)}, bf16[128,128]{1,0:T(8,128)(2,1)}, u32[]{:S(2)}) copy-start(bf16[128,128]{1,0:T(8,128)(2,1)} %param.20) | copy-start | bytes 98308
  0.0 11.0 %copy-start.8 = (bf16[128]{0:T(256)(128)(2,1)S(1)}, bf16[128]{0:T(256)(128)(2,1)}, u32[]{:S(2)}) copy-start(bf16[128]{0:T(256)(128)(2,1)} %param.14) | copy-start | bytes 772
  0.0 11.0 %copy-start.9 = (bf16[128]{0:T(256)(128)(2,1)S(1)}, bf16[128]{0:T(256)(128)(2,1)}, u32[]{:S(2)}) copy-start(bf16[128]{0:T(256)(128)(2,1)} %param.15) | copy-start | bytes 772
  0.0 11.0 %copy-start.3 = (bf16[128,128]{1,0:T(8,128)(2,1)S(1)}, bf16[128,128]{1,0:T(8,128)(2,1)}, u32[]{:S(2)}) copy-start(bf16[128,128]{1,0:T(8,128)(2,1)} %param.16) | copy-start | bytes 98308
  0.0 11.2 %copy-start.4 = (bf16[128,128]{1,0:T(8,128)(2,1)S(1)}, bf16[128,128]{1,0:T(8,128)(2,1)}, u32[]{:S(2)}) copy-start(bf16[128,128]{1,0:T(8,128)(2,1)} %param.17) | copy-start | bytes 98308
  0.0 11.3 %copy-start.5 = (bf16[128,128]{1,0:T(8,128)(2,1)S(1)}, bf16[128,128]{1,0:T(8,128)(2,1)}, u32[]{:S(2)}) copy-start(bf16[128,128]{1,0:T(8,128)(2,1)} %param.18) | copy-start | bytes 98308
  0.0 11.4 %copy-start.6 = (bf16[128,128]{1,0:T(8,128)(2,1)S(1)}, bf16[128,128]{1,0:T(8,128)(2,1)}, u32[]{:S(2)}) copy-start(bf16[128,128]{1,0:T(8,128)(2,1)} %param.19) | copy-start | bytes 98308
  0.1 11.5 %copy-start.2 = (s32[12,1536]{1,0:T(8,128)S(1)}, s32[12,1536]{1,0:T(8,128)}, u32[]{:S(2)}) copy-start(s32[12,1536]{1,0:T(8,128)} %param.13) | copy-start | bytes 221188
  48.7 102.2 %all-to-all-start = ((bf16[128,12,1536]{2,1,0:T(8,128)(2,1)}), bf16[128,12,1536]{2,1,0:T(8,128)(2,1)}, u32[]{:S(2)}, u32[]{:S(2)}) async-start(bf16[128,12,1536]{2,1,0:T(8,128)(2,1)} %copy.29), calls=%async_computation | async-start | bytes 12582912 | tf_op jit(solution)/shard_map/all_to_all | solution.py:43
  150.9 89.4 %all-to-all-start.1 = ((bf16[128,12,1536]{2,1,0:T(8,128)(2,1)}), bf16[128,12,1536]{2,1,0:T(8,128)(2,1)}, u32[]{:S(2)}, u32[]{:S(2)}) async-start(bf16[128,12,1536]{2,1,0:T(8,128)(2,1)} %copy.30), calls=%async_computation.1 | async-start | bytes 12582912 | tf_op jit(solution)/shard_map/all_to_all | solution.py:44
  343.9 25.6 %copy-start.10 = (bf16[128]{0:T(256)(128)(2,1)S(1)}, bf16[128]{0:T(256)(128)(2,1)}, u32[]{:S(2)}) copy-start(bf16[128]{0:T(256)(128)(2,1)} %param.21) | copy-start | bytes 772
  343.9 25.6 %copy-start.11 = (bf16[128]{0:T(256)(128)(2,1)S(1)}, bf16[128]{0:T(256)(128)(2,1)}, u32[]{:S(2)}) copy-start(bf16[128]{0:T(256)(128)(2,1)} %param.22) | copy-start | bytes 772
  355.3 81.0 %all-to-all-start.2 = ((bf16[128,2,9216]{2,1,0:T(2,128)(2,1)}), bf16[128,2,9216]{2,1,0:T(2,128)(2,1)}, u32[]{:S(2)}, u32[]{:S(2)}) async-start(bf16[128,2,9216]{2,1,0:T(2,128)(2,1)} %reshape.71), calls=%async_computation.2 | async-start | bytes 9437184 | tf_op jit(solution)/shard_map/all_to_all | solution.py:46
  505.2 8.2 %copy-start.1 = (f32[128,12,1536]{2,1,0:T(8,128)S(1)}, f32[128,12,1536]{2,1,0:T(8,128)}, u32[]{:S(2)}) copy-start(f32[128,12,1536]{2,1,0:T(8,128)} %reshape.66) | copy-start | bytes 28311556
  505.2 13.3 %slice-start = ((s8[4718592]{0:T(1024)(128)(4,1)}), s8[4194304]{0:T(1024)(128)(4,1)S(1)}, s32[]{:S(2)}) async-start(s8[4718592]{0:T(1024)(128)(4,1)} %bitcast.18), calls=%async_computation.3 | async-start | bytes 8388608
  513.3 5.1 slice-start.1
  513.3 5.1 copy-start.7
where the time goes:
time: 543 us; the launch traced here: 533 us
  waiting for transfers between devices  213 us (39%)
  local copies, waits for them, and re-layouts  127 us (23%)
  other arithmetic  108 us (20%)
  matrix products  50.7 us (9%)
  starting transfers between devices  33.5 us (6%)
    all_to_all x1, waiting for transfers between devices, local_fn(): a_chan = lax.all_to_all(a_side, 'dap', 0, 1, tiled=True)  82.3 us
    all_to_all x1, waiting for transfers between devices, local_fn(): b_chan = lax.all_to_all(b_side, 'dap', 0, 1, tiled=True)  74.1 us
    all_to_all x1, waiting for transfers between devices, local_fn(): tri_rows = lax.all_to_all(tri_chan, 'dap', 1, 0, tiled=True)  56.9 us
    convert_element_type x1, local copies, waits for them, and re-layouts, local_fn(): jnp.einsum('cik,cjk->cij', a_chan, b_chan, preferred_element_type=jnp.flo...  52.2 us
    unnamed x35, local copies, waits for them, and re-layouts  34 us
    convert_element_type x1, other arithmetic, finish_rows(): tri_rows.astype(jnp.float32)  32.3 us
    unnamed x2, other arithmetic  31.8 us
    convert_element_type x1, other arithmetic, gated_pair(): (mask_f * jax.nn.sigmoid(projected[3]) * projected[2]).astype(jnp.bfloat16)  16.4 us
  transfers between devices with their start and end apart: 3, of which 3 were waited for; matrix products, arithmetic and copies ran while one was open for 5% of the time, Pallas kernels for 0%

commit v1 on v0

v1 whole, which is shorter than its diff:
```python
import functools

import jax
import jax.numpy as jnp
from jax import lax
from jax.experimental import pallas as pl
from jax.experimental.pallas import tpu as pltpu
from jax.sharding import PartitionSpec as P

LN_EPS = 1e-5
MESH = pl.DeviceIdType.MESH
DMA = pltpu.SemaphoreType.DMA
VMEM = pltpu.VMEM
ANY = pl.ANY
N = 1536
C = 128
SIDE = 4
CH = 64
RL = 12
TR = 8
NG = 3
KC = 256
HALF = N // 2
SKEW = 9
YSK = 129
BF = jnp.bfloat16
F32 = jnp.float32


def place():
    me = lax.axis_index('dap')
    chip, core = me // 2, me % 2
    return core, (chip // 16, (chip // 4) % 4, chip % 4)


def dev(coords, core):
    return {'dap': (coords[0] * 16 + coords[1] * 4 + coords[2]) * 2 + core}


def shift(coords, dim, by):
    return tuple((v + by) % SIDE if i == dim else v for i, v in enumerate(coords))


def pick(dim, at):
    return tuple(at if i == dim else slice(None) for i in range(3))


def enter(core, coords):
    barrier = pltpu.get_barrier_semaphore()
    for dim in range(3):
        for by in range(1, SIDE):
            pl.semaphore_signal(barrier, inc=1, device_id=dev(shift(coords, dim, by), core), device_id_type=MESH)
    pl.semaphore_signal(barrier, inc=1, device_id=dev(coords, 1 - core), device_id_type=MESH)
    pl.semaphore_wait(barrier, 3 * (SIDE - 1) + 1)


def wait_bytes(ref, sem):
    pltpu.make_async_copy(ref, ref, sem).wait()


def send_phase(core, coords, dim, src_at, dst_at, ssem, rsem):
    for by in (1, 3, 2):
        to = (coords[dim] + by) % SIDE
        pltpu.make_async_remote_copy(
            src_ref=src_at(pick(dim, to)), dst_ref=dst_at(pick(dim, coords[dim])), send_sem=ssem, recv_sem=rsem,
            device_id=dev(shift(coords, dim, by), core), device_id_type=MESH).start()


def keep_own(coords, dim, src, dst, lead):
    def body(i, carry):
        idx = [i // SIDE, i % SIDE]
        idx.insert(dim, coords[dim])
        at = lead + tuple(idx)
        dst[at] = src[at]
        return carry
    lax.fori_loop(0, SIDE * SIDE, body, 0)


def sigmoid(v):
    return 0.5 * jnp.tanh(0.5 * v) + 0.5


def pairs_kernel(z_hbm, mask_ref, scale_ref, bias_ref, wa_ref, wag_ref, wb_ref, wbg_ref, b_out, a_out, x_out,
                 zbuf, xall, mall, wt, stage_a, stage_b, sa, sb, r1a, r1b, r2a, r2b,
                 zsem, xssem, xrsem, mrsem, msem, xosem, ssem, rsem, fsem):
    core, coords = place()
    for r in range(RL):
        pltpu.make_async_copy(z_hbm.at[r], zbuf.at[r], zsem.at[r]).start()
    for i, w in enumerate((wa_ref, wag_ref, wb_ref, wbg_ref)):
        wt[i] = w[...].astype(F32).T.astype(BF)
    mall[core] = mask_ref[...]
    enter(core, coords)
    partner = dev(coords, 1 - core)
    mcopy = pltpu.make_async_remote_copy(src_ref=mask_ref, dst_ref=mall.at[core], send_sem=msem, recv_sem=mrsem,
                                         device_id=partner, device_id_type=MESH)
    mcopy.start()
    scale = scale_ref[...].astype(F32)
    bias = bias_ref[...].astype(F32)

    def norm_row(r, carry):
        wait_bytes(zbuf.at[0], zsem.at[r])
        row = core * RL + r

        def chunk(i, carry):
            at = pl.ds(pl.multiple_of(i * KC, KC), KC)
            v = zbuf[r, at, :].astype(F32)
            centered = v - jnp.mean(v, axis=-1, keepdims=True)
            var = jnp.mean(centered * centered, axis=-1, keepdims=True)
            xall[row, at, :] = (centered * lax.rsqrt(var + LN_EPS) * scale + bias).astype(BF)
            return carry
        lax.fori_loop(0, N // KC, chunk, 0)
        pltpu.make_async_remote_copy(src_ref=xall.at[row], dst_ref=xall.at[row], send_sem=xssem, recv_sem=xrsem.at[r],
                                     device_id=partner, device_id_type=MESH).start()
        pltpu.make_async_copy(xall.at[row], x_out.at[r], xosem).start()
        return carry
    lax.fori_loop(0, RL, norm_row, 0)
    mcopy.wait()

    half = pl.ds(pl.multiple_of(core * CH, CH), CH)
    wcat = jnp.concatenate([wt[i, half, :] for i in range(4)], axis=0)
    send = [(sb, r1b, r2b, 0), (sa, r1a, r2a, 1)]

    def phase(arr, g, ph):
        s, r1, r2, k = send[arr]
        dim = (g + ph) % 3
        src = (s, r1, r2)[ph]
        if ph < 2:
            dst = (r1, r2)[ph]
            send_phase(core, coords, dim, lambda p: src.at[(g,) + p], lambda p: dst.at[(g,) + p], ssem, rsem.at[k, g, ph])
            keep_own(coords, dim, src, dst, (g,))
        else:
            def final(p):
                return b_out.at[p + (g,)] if k == 0 else a_out.at[(g,) + p]
            send_phase(core, coords, dim, lambda p: src.at[(g,) + p], final, ssem, rsem.at[k, g, ph])
            own = pick(dim, coords[dim])
            pltpu.make_async_copy(src.at[(g,) + own], final(own), fsem).start()

    def arrived(arr, g, ph):
        s, r1, r2, k = send[arr]
        wait_bytes(r1.at[g, pl.ds(0, 3)], rsem.at[k, g, ph])

    for g in range(NG):
        def project_row(i, carry):
            row = g * TR + i
            owner, within = row // RL, row % RL

            @pl.when(owner != core)
            def _():
                wait_bytes(xall.at[0], xrsem.at[within])

            for j in range(N // KC):
                at = pl.ds(j * KC, KC)
                p = lax.dot_general(wcat, xall[row, at, :], (((1,), (1,)), ((), ())), preferred_element_type=F32)
                keep = mall[owner, pl.ds(within, 1), at].astype(F32)
                a = sigmoid(p[CH:2 * CH]) * p[:CH] * keep
                b = sigmoid(p[3 * CH:]) * p[2 * CH:3 * CH] * keep
                for t in range(KC // 128):
                    lanes = slice(t * 128, (t + 1) * 128)
                    kt = j * (KC // 128) + t
                    stage_a[kt, pl.ds(i, CH, stride=SKEW), :] = a[:, lanes]
                    stage_b[kt, pl.ds(i, CH, stride=SKEW), :] = b[:, lanes]
            return carry
        lax.fori_loop(0, TR, project_row, 0)

        def pack(c, carry):
            at = (g, c // 16, (c // 4) % 4, c % 4)
            for stage, s in ((stage_b, sb), (stage_a, sa)):
                for j in range(N // KC):
                    v = jnp.concatenate([stage[2 * j + t, pl.ds(c * SKEW, TR), :] for t in range(2)], axis=1)
                    s[at + (slice(None), pl.ds(j * KC, KC))] = v.astype(BF)
            return carry
        lax.fori_loop(0, CH, pack, 0)
        phase(0, g, 0)

    for g in range(NG):
        phase(1, g, 0)
    for ph in (1, 2):
        for arr in range(2):
            for g in range(NG):
                arrived(arr, g, ph - 1)
                phase(arr, g, ph)
    for arr in range(2):
        for g in range(NG):
            arrived(arr, g, 2)
    for _ in range(6):
        wait_bytes(r1a.at[:, pl.ds(0, 3)], ssem)
    for _ in range(2):
        wait_bytes(r1a.at[:, 0], fsem)
    wait_bytes(zbuf, xosem)
    wait_bytes(zbuf, xssem)


def triangle_kernel(a_hbm, b_hbm, own_out, par_out, abuf, bbuf, t, r1, r2, lsem, ssem, rsem, fsem, dssem, drsem):
    core, coords = place()
    bcopy = pltpu.make_async_copy(b_hbm, bbuf, lsem.at[NG])
    acopy = [pltpu.make_async_copy(a_hbm.at[g], abuf.at[g], lsem.at[g]) for g in range(NG)]
    bcopy.start()
    for cp in acopy:
        cp.start()
    enter(core, coords)
    bcopy.wait()

    def phase(g, h, ph):
        dim = (g + ph) % 3
        src = (t, r1, r2)[ph]
        if ph < 2:
            dst = (r1, r2)[ph]
            send_phase(core, coords, dim, lambda p: src.at[(g, h) + p], lambda p: dst.at[(g, h) + p], ssem, rsem.at[g, h, ph])
            keep_own(coords, dim, src, dst, (g, h))
        else:
            def final(p):
                return own_out.at[p + (g, slice(None), pl.ds(h * HALF, HALF))]
            send_phase(core, coords, dim, lambda p: src.at[(g, h) + p], final, ssem, rsem.at[g, h, ph])
            own = pick(dim, coords[dim])
            pltpu.make_async_copy(src.at[(g, h) + own], final(own), fsem.at[h]).start()

    def arrived(g, h, ph):
        wait_bytes(r1.at[g, h, pl.ds(0, 3)], rsem.at[g, h, ph])

    for h in range(2):
        for g in range(NG):
            if h == 0:
                acopy[g].wait()

            for n in range(HALF // KC):
                acc = lax.dot_general(abuf[g], bbuf[pl.ds(h * HALF + n * KC, KC), :], (((1,), (1,)), ((), ())),
                                      preferred_element_type=F32)
                t[g, h, :, :, :, :, pl.ds(n * KC, KC)] = acc.astype(BF).reshape(SIDE, SIDE, SIDE, TR, KC)
            phase(g, h, 0)
    for ph in (1, 2):
        for h in range(2):
            for g in range(NG):
                arrived(g, h, ph - 1)
                phase(g, h, ph)
    swaps = []
    for h in range(2):
        for g in range(NG):
            arrived(g, h, 2)
        wait_bytes(r1.at[:, 0, 0], fsem.at[h])
        cols = pl.ds(h * HALF, HALF)
        swap = pltpu.make_async_remote_copy(
            src_ref=own_out.at[:, :, :, pl.ds(1 - core, 2), :, cols], dst_ref=par_out.at[:, :, :, :, :, cols],
            send_sem=dssem.at[h], recv_sem=drsem.at[h], device_id=dev(coords, 1 - core), device_id_type=MESH)
        swap.start()
        swaps.append(swap)
    for swap in swaps:
        swap.wait()
    for _ in range(3):
        wait_bytes(r1.at[:, :, pl.ds(0, 3)], ssem)


def finish_kernel(hid_ref, town, tpar, x_ref, z_ref, wg_ref, wo_ref, out_ref, y):
    core = lax.axis_index('dap') % 2
    step = 8

    def own(c):
        return town[pl.ds(c, step), pl.ds(core, 2), :, :].astype(F32)

    def par(c):
        return tpar[pl.ds(c, step), :, :, :].astype(F32)

    def add(i, acc):
        c = i * step
        return acc + jnp.sum(own(c), axis=0) + jnp.sum(par(c), axis=0)
    zero = jnp.zeros((2, TR, KC), F32)
    mean = lax.fori_loop(0, CH // step, add, zero) * (1.0 / C)

    def add_sq(i, acc):
        c = i * step
        u, v = own(c) - mean, par(c) - mean
        return acc + jnp.sum(u * u, axis=0) + jnp.sum(v * v, axis=0)
    var = lax.fori_loop(0, CH // step, add_sq, zero) * (1.0 / C)
    rstd = lax.rsqrt(var + LN_EPS)

    def spread(i, carry):
        for first, vals in ((core * CH, own(i * step)), ((1 - core) * CH, par(i * step))):
            for k in range(step):
                c = first + i * step + k
                v = (vals[k] - mean) * rstd * hid_ref[0, c] + hid_ref[1, c]
                for tile in range(2):
                    for lt in range(KC // 128):
                        y[lt, pl.ds(tile * TR * YSK + c, TR, stride=YSK), :] = v[tile, :, lt * 128:(lt + 1) * 128]
        return carry
    lax.fori_loop(0, CH // step, spread, 0)

    def row(r, carry):
        at = pl.ds((r + 4 * core) * YSK, C)
        yt = jnp.concatenate([y[lt, at, :] for lt in range(KC // 128)], axis=1).astype(BF)
        update = lax.dot_general(yt, wo_ref[...], (((0,), (0,)), ((), ())), preferred_element_type=F32)
        gate = sigmoid(jnp.dot(x_ref[r], wg_ref[...], preferred_element_type=F32))
        out_ref[r] = (z_ref[r].astype(F32) + gate * update).astype(BF)
        return carry
    lax.fori_loop(0, RL, row, 0)


def solution(mesh):
    row_spec = P(('data', 'dap'), None, None)
    mask_spec = P(('data', 'dap'), None)
    replicated = P()
    vspec = pl.BlockSpec(memory_space=VMEM)
    aspec = pl.BlockSpec(memory_space=ANY)

    def local_fn(z_loc, mask_loc, ln_scale, ln_bias, w_a, w_a_gate, w_b, w_b_gate, w_gate, ln_hid_scale, ln_hid_bias, w_out):
        sets = (NG, SIDE, SIDE, SIDE, TR, N)
        chips = (SIDE, SIDE, SIDE, NG, TR, N)
        b_all, a_all, x_norm = pl.pallas_call(
            pairs_kernel, name='pairs',
            out_shape=(jax.ShapeDtypeStruct(chips, BF), jax.ShapeDtypeStruct(sets, BF), jax.ShapeDtypeStruct((RL, N, C), BF)),
            in_specs=[aspec] + [vspec] * 7, out_specs=(aspec,) * 3,
            scratch_shapes=[
                VMEM((RL, N, C), BF), VMEM((2 * RL, N, C), BF), VMEM((2, RL, N), jnp.int32), VMEM((4, C, C), BF),
                VMEM((N // 128, CH * SKEW, 128), F32), VMEM((N // 128, CH * SKEW, 128), F32),
                VMEM(sets, BF), VMEM(sets, BF), VMEM(sets, BF), VMEM(sets, BF), VMEM(sets, BF), VMEM(sets, BF),
                DMA((RL,)), DMA, DMA((RL,)), DMA, DMA, DMA, DMA, DMA((2, NG, 3)), DMA],
            compiler_params=pltpu.CompilerParams(collective_id=1, has_side_effects=True, vmem_limit_bytes=64 * 2**20 - 65536),
        )(z_loc, mask_loc, ln_scale.reshape(1, C), ln_bias.reshape(1, C), w_a, w_a_gate, w_b, w_b_gate)
        units = (NG, 2, SIDE, SIDE, SIDE, TR, HALF)
        own, par = pl.pallas_call(
            triangle_kernel, name='triangle',
            out_shape=(jax.ShapeDtypeStruct(chips, BF), jax.ShapeDtypeStruct((SIDE, SIDE, SIDE, 2, TR, N), BF)),
            in_specs=[aspec] * 2, out_specs=(aspec,) * 2,
            scratch_shapes=[VMEM((NG, CH * TR, N), BF), VMEM((N, N), BF), VMEM(units, BF), VMEM(units, BF), VMEM(units, BF),
                            DMA((NG + 1,)), DMA, DMA((NG, 2, 3)), DMA((2,)), DMA((2,)), DMA((2,))],
            compiler_params=pltpu.CompilerParams(collective_id=2, has_side_effects=True, vmem_limit_bytes=60 * 2**20),
        )(a_all.reshape(NG, CH * TR, N), b_all.reshape(N, N))
        hid = jnp.stack([ln_hid_scale, ln_hid_bias]).astype(F32)
        wspec = pl.BlockSpec((C, C), lambda j: (0, 0))
        rspec = pl.BlockSpec((RL, KC, C), lambda j: (0, j, 0))
        return pl.pallas_call(
            finish_kernel, name='finish', grid=(N // KC,),
            out_shape=jax.ShapeDtypeStruct((RL, N, C), BF),
            in_specs=[pl.BlockSpec(memory_space=pltpu.SMEM),
                      pl.BlockSpec((CH, NG, TR, KC), lambda j: (0, 0, 0, j)), pl.BlockSpec((CH, 2, TR, KC), lambda j: (0, 0, 0, j)),
                      rspec, rspec, wspec, wspec],
            out_specs=rspec,
            scratch_shapes=[VMEM((KC // 128, 2 * TR * YSK, 128), F32)],
            compiler_params=pltpu.CompilerParams(vmem_limit_bytes=48 * 2**20),
        )(hid, own.reshape(CH, NG, TR, N), par.reshape(CH, 2, TR, N), x_norm, z_loc, w_gate, w_out)

    return jax.shard_map(local_fn, mesh=mesh, in_specs=(row_spec, mask_spec) + (replicated,) * 10, out_specs=row_spec, check_vma=False)
```

time: 543 us -> 231 us (0.43); the launches traced: 533 us -> 231 us
  Pallas kernels: 0 us -> 229 us
  waiting for transfers between devices: 213 us -> 0 us
  local copies, waits for them, and re-layouts: 127 us -> 1.91 us
  other arithmetic: 108 us -> 0.01 us
  matrix products: 50.7 us -> 0 us
  starting transfers between devices: 33.5 us -> 0 us
    pallas_call x0 -> x3, Pallas kernels: none -> 229 us  [the longest x1 139 us: local_fn(): pl.pallas_call(pairs_kernel, name='pairs', out_shape=(jax.ShapeDtypeStruc...]
    all_to_all x3 -> x0, waiting for transfers between devices: 213 us -> none  [the longest x1 82.3 us: local_fn(): a_chan = lax.all_to_all(a_side, 'dap', 0, 1, tiled=True)]
    convert_element_type x4 -> x0, local copies, waits for them, and re-layouts: 76.5 us -> none  [the longest x1 52.2 us: local_fn(): jnp.einsum('cik,cjk->cij', a_chan, b_chan, preferred_element_type=jnp.flo...]
    convert_element_type x8 -> x1, other arithmetic: 53.9 us -> 0.01 us  [local_fn(): hid = jnp.stack([ln_hid_scale, ln_hid_bias]).astype(F32)]
    dot_general x4 -> x0, matrix products: 50.7 us -> none  [the longest x1 15.4 us: gated_pair(): jnp.einsum('rkd,de->erk', x_norm, w_cat, preferred_element_type=jnp.float32)]
    all_to_all x3 -> x0, starting transfers between devices: 33.5 us -> none  [the longest x1 14.1 us: local_fn(): tri_rows = lax.all_to_all(tri_chan, 'dap', 1, 0, tiled=True)]
    unnamed x35 -> x10, local copies, waits for them, and re-layouts: 34 us -> 1.91 us
    unnamed x2 -> x0, other arithmetic: 31.8 us -> none
  transfers between devices with their start and end apart: 3 -> 0, of which waited for: 3 -> 0; matrix products, arithmetic and copies ran while one was open for 5% -> 0% of each run, Pallas kernels for 0% -> 0%
where the time goes in v1:
time: 231 us
  Pallas kernels  229 us (99%)
    pallas_call x1, Pallas kernels, local_fn(): pl.pallas_call(pairs_kernel, name='pairs', out_shape=(jax.ShapeDtypeStruc...  139 us
    pallas_call x1, Pallas kernels, local_fn(): pl.pallas_call(triangle_kernel, name='triangle', out_shape=(jax.ShapeDtyp...  65.1 us
    pallas_call x1, Pallas kernels, local_fn(): pl.pallas_call(finish_kernel, name='finish', grid=(N // KC,), out_shape=j...  24.4 us

profile of v1, /device:TPU:1, one launch (start us, length us, event | category | flops | bytes accessed | tf_op | source)
XLA Modules:
  0.0 230.7 jit_solution(284625372319928936)
XLA Ops:
  0.0 139.2 %pairs.1 = (bf16[4,4,4,3,8,1536]{5,4,3,2,1,0:T(8,128)(2,1)}, bf16[3,4,4,4,8,1536]{5,4,3,2,1,0:T(8,128)(2,1)}, bf16[12,1536,128]{2,1,0:T(8,128)(2,1)}) custom-call(bf16[12,1536,128]{2,1,0:T(8,128)(2,1)} %z_ref.1, s32[12,1536]{1,0:T(8,128)} %mask_ref.1, bf16[1,128]{1,0:T(2,128)(2,1)} %bitcast.14, bf16[1,128]{1,0:T(2,128)(2,1)} %bitcast.15, ...), custom_call_target="tpu_custom_call" | custom-call | tf_op jit(solution)/shard_map/pairs/pallas_call | solution.py:306
  139.2 0.0 copy-start.3
  139.2 0.0 copy-start.4
  139.2 0.0 copy-start.1
  139.2 0.0 copy-start.2
  139.3 65.1 %triangle.1 = (bf16[4,4,4,3,8,1536]{5,4,3,2,1,0:T(8,128)(2,1)}, bf16[4,4,4,2,8,1536]{5,4,3,2,1,0:T(8,128)(2,1)}) custom-call(bf16[3,512,1536]{2,1,0:T(8,128)(2,1)} %bitcast.10, bf16[1536,1536]{1,0:T(8,128)(2,1)} %bitcast.9), custom_call_target="tpu_custom_call" | custom-call | tf_op jit(solution)/shard_map/triangle/pallas_call | solution.py:318
  204.4 0.0 copy-done.3
  204.4 0.0 copy-done.4
  204.4 0.0 copy-done.1
  204.4 0.0 copy-done.2
  204.4 0.0 copy-start
  204.4 1.9 copy-done
  206.3 24.4 %finish.1 = bf16[12,1536,128]{2,1,0:T(8,128)(2,1)} custom-call(f32[2,128]{1,0:T(2,128)S(1)} %maximum_convert_fusion.hid_ref, bf16[64,3,8,1536]{3,2,1,0:T(8,128)(2,1)} %bitcast.11, bf16[64,2,8,1536]{3,2,1,0:T(8,128)(2,1)S(1)} %bitcast.8, bf16[12,1536,128]{2,1,0:T(8,128)(2,1)} %get-tuple-element.14.x_ref, bf16[12,1536,128]{2,1,0:T(8,128)(2,1)} %z_ref.1, ...), custom_call_target="tpu_custom_call" | custom-call | tf_op jit(solution)/shard_map/finish/pallas_call | solution.py:329
  (1 shorter events, 0.0 us)
Async XLA Ops:
  139.2 65.1 %copy-start.3 = (bf16[128]{0:T(256)(128)(2,1)S(1)}, bf16[128]{0:T(256)(128)(2,1)}, u32[]{:S(2)}) copy-start(bf16[128]{0:T(256)(128)(2,1)} %param.22) | copy-start | bytes 772
  139.2 65.1 %copy-start.4 = (bf16[128]{0:T(256)(128)(2,1)S(1)}, bf16[128]{0:T(256)(128)(2,1)}, u32[]{:S(2)}) copy-start(bf16[128]{0:T(256)(128)(2,1)} %param.21) | copy-start | bytes 772
  139.2 65.2 %copy-start.1 = (bf16[128,128]{1,0:T(8,128)(2,1)S(1)}, bf16[128,128]{1,0:T(8,128)(2,1)}, u32[]{:S(2)}) copy-start(bf16[128,128]{1,0:T(8,128)(2,1)} %wg_ref.1) | copy-start | bytes 98308
  139.2 65.2 %copy-start.2 = (bf16[128,128]{1,0:T(8,128)(2,1)S(1)}, bf16[128,128]{1,0:T(8,128)(2,1)}, u32[]{:S(2)}) copy-start(bf16[128,128]{1,0:T(8,128)(2,1)} %wo_ref.1) | copy-start | bytes 98308
  204.4 1.9 copy-start

commit v2 on v0

v2 whole, which is shorter than its diff:
```python
import functools

import jax
import jax.numpy as jnp
from jax import lax
from jax.experimental import pallas as pl
from jax.experimental.pallas import tpu as pltpu
from jax.sharding import PartitionSpec as P

LN_EPS = 1e-5
MESH = pl.DeviceIdType.MESH
DMA = pltpu.SemaphoreType.DMA
VMEM = pltpu.VMEM
ANY = pl.ANY
N = 1536
C = 128
SIDE = 4
CH = 64
RL = 12
TR = 8
NG = 3
KC = 256
NT = 3
KT = N // NT
NQ = 4
KQ = N // NQ
SKEW = 9
YSK = 129
BF = jnp.bfloat16
F32 = jnp.float32


def place():
    me = lax.axis_index('dap')
    chip, core = me // 2, me % 2
    return core, (chip // 16, (chip // 4) % 4, chip % 4)


def dev(coords, core):
    return {'dap': (coords[0] * 16 + coords[1] * 4 + coords[2]) * 2 + core}


def shift(coords, dim, by):
    return tuple((v + by) % SIDE if i == dim else v for i, v in enumerate(coords))


def pick(dim, at):
    return tuple(at if i == dim else slice(None) for i in range(3))


def greet(sem, core, coords):
    for dim in range(3):
        for by in range(1, SIDE):
            pl.semaphore_signal(sem, inc=1, device_id=dev(shift(coords, dim, by), core), device_id_type=MESH)
    pl.semaphore_signal(sem, inc=1, device_id=dev(coords, 1 - core), device_id_type=MESH)


GREETED = 3 * (SIDE - 1) + 1


def wait_bytes(ref, sem):
    pltpu.make_async_copy(ref, ref, sem).wait()


def send_phase(core, coords, dim, src_at, dst_at, ssem, rsem):
    for by in (1, 3, 2):
        to = (coords[dim] + by) % SIDE
        pltpu.make_async_remote_copy(
            src_ref=src_at(pick(dim, to)), dst_ref=dst_at(pick(dim, coords[dim])), send_sem=ssem, recv_sem=rsem,
            device_id=dev(shift(coords, dim, by), core), device_id_type=MESH).start()


def keep_own(coords, dim, src, src_at, dst, dst_at):
    def body(i, carry):
        idx = [i // SIDE, i % SIDE]
        idx.insert(dim, coords[dim])
        idx = tuple(idx)
        dst[dst_at(idx)] = src[src_at(idx)]
        return carry
    lax.fori_loop(0, SIDE * SIDE, body, 0)


def sigmoid(v):
    return 0.5 * jnp.tanh(0.5 * v) + 0.5


def update_kernel(hid_ref, z_hbm, mask_ref, scale_ref, bias_ref, wa_ref, wag_ref, wb_ref, wbg_ref, wg_ref, wo_ref, out_hbm,
                  zbuf, xall, mall, wt, stage_a, stage_b, sa, sb, r1a, r1b, r2a, r2b, aa, bb, y, obuf,
                  zsem, xssem, xown, xmix, mrsem, msem, ssem, rsem, tssem, trsem, dssem, drsem, osem, credit):
    core, coords = place()
    barrier = pltpu.get_barrier_semaphore()
    greet(barrier, core, coords)
    partner = dev(coords, 1 - core)
    own0, mix0 = 4 * core, 8 - 8 * core
    tile = [s + core * (2 - 2 * s) for s in range(NG)]
    full = slice(None)

    def kcols(t):
        return pl.ds(t * KT, KT)

    def qcols(q):
        return pl.ds(q * KQ, KQ)

    loads = [pltpu.make_async_copy(z_hbm.at[pl.ds(own0, TR), kcols(t)], zbuf.at[pl.ds(own0, TR), kcols(t)], zsem.at[t])
             for t in range(NT)]
    loads.append(pltpu.make_async_copy(z_hbm.at[pl.ds(mix0, 4)], zbuf.at[pl.ds(mix0, 4)], zsem.at[NT]))
    for cp in loads:
        cp.start()
    for i, w in enumerate((wa_ref, wag_ref, wb_ref, wbg_ref)):
        wt[i] = w[...].astype(F32).T.astype(BF)
    mall[core] = mask_ref[...]
    scale = scale_ref[...].astype(F32)
    bias = bias_ref[...].astype(F32)
    half = pl.ds(pl.multiple_of(core * CH, CH), CH)
    wcat = jnp.concatenate([wt[i, half, :] for i in range(4)], axis=0)

    def norm(first, rows, t):
        def body(i, carry):
            r = first + i
            for k in range(KT // KC):
                at = pl.ds(t * KT + k * KC, KC)
                v = zbuf[r, at, :].astype(F32)
                centered = v - jnp.mean(v, axis=-1, keepdims=True)
                var = jnp.mean(centered * centered, axis=-1, keepdims=True)
                xall[core * RL + r, at, :] = (centered * lax.rsqrt(var + LN_EPS) * scale + bias).astype(BF)
            return carry
        lax.fori_loop(0, rows, body, 0)

    def give_x(first, rows, t, rsem_x):
        block = xall.at[pl.ds(core * RL + first, rows), kcols(t)]
        pltpu.make_async_remote_copy(src_ref=block, dst_ref=block, send_sem=xssem, recv_sem=rsem_x.at[t],
                                     device_id=partner, device_id_type=MESH).start()

    bufs = ((sb, r1b, r2b), (sa, r1a, r2a))

    def phase(arr, s, t, ph):
        dim = (s + t + ph) % 3
        src = bufs[arr][ph]

        def at(p):
            return (s,) + p + (full, kcols(t))

        def final(p):
            return p + (tile[s], full, kcols(t)) if arr == 0 else at(p)
        dst = (bb, aa)[arr] if ph == 2 else bufs[arr][ph + 1]
        dst_at = final if ph == 2 else at
        send_phase(core, coords, dim, lambda p: src.at[at(p)], lambda p: dst.at[dst_at(p)], ssem.at[arr, ph],
                   rsem.at[arr, s, t, ph])
        keep_own(coords, dim, src, at, dst, dst_at)

    def arrived(arr, s, t, ph):
        wait_bytes(r1a.at[s, pl.ds(0, 3), full, full, full, kcols(t)], rsem.at[arr, s, t, ph])

    def make_unit(s, t):
        def project_row(i, carry):
            row = tile[s] * TR + i
            owner, within = row // RL, row % RL
            for j in range(KT // KC):
                at = pl.ds(t * KT + j * KC, KC)
                p = lax.dot_general(wcat, xall[row, at, :], (((1,), (1,)), ((), ())), preferred_element_type=F32)
                keep = mall[owner, pl.ds(within, 1), at].astype(F32)
                a = sigmoid(p[CH:2 * CH]) * p[:CH] * keep
                b = sigmoid(p[3 * CH:]) * p[2 * CH:3 * CH] * keep
                for u in range(KC // 128):
                    lanes = slice(u * 128, (u + 1) * 128)
                    kt = j * (KC // 128) + u
                    stage_a[kt, pl.ds(i, CH, stride=SKEW), :] = a[:, lanes]
                    stage_b[kt, pl.ds(i, CH, stride=SKEW), :] = b[:, lanes]
            return carry
        lax.fori_loop(0, TR, project_row, 0)
        for arr, stage in ((0, stage_b), (1, stage_a)):
            s_ref = bufs[arr][0]

            def pack(c, carry):
                at = (s, c // 16, (c // 4) % 4, c % 4)
                for j in range(KT // KC):
                    v = jnp.concatenate([stage[2 * j + u, pl.ds(c * SKEW, TR), :] for u in range(2)], axis=1)
                    s_ref[at + (full, pl.ds(t * KT + j * KC, KC))] = v.astype(BF)
                return carry
            lax.fori_loop(0, CH, pack, 0, unroll=4)
            phase(arr, s, t, 0)

    for t in range(NT):
        loads[t].wait()
        norm(own0, TR, t)
        if t == 0:
            pl.semaphore_wait(barrier, GREETED)
            mcopy = pltpu.make_async_remote_copy(src_ref=mask_ref, dst_ref=mall.at[core], send_sem=msem, recv_sem=mrsem,
                                                 device_id=partner, device_id_type=MESH)
            mcopy.start()
        give_x(own0, TR, t, xown)
        make_unit(0, t)
    loads[NT].wait()
    for t in range(NT):
        norm(mix0, 4, t)
        give_x(mix0, 4, t, xmix)
    mcopy.wait()
    for s in (1, 2):
        for t in range(NT):
            if s == 1:
                wait_bytes(xall.at[pl.ds(0, 4), kcols(t)], xmix.at[t])
            else:
                wait_bytes(xall.at[pl.ds(0, TR), kcols(t)], xown.at[t])
            make_unit(s, t)

    for ph in (1, 2):
        for arr in range(2):
            for s in range(NG):
                for t in range(NT):
                    arrived(arr, s, t, ph - 1)
                    phase(arr, s, t, ph)
    for arr, ph in ((0, 0), (1, 0), (0, 1), (1, 1), (0, 2)):
        wait_bytes(r1a.at[:, pl.ds(0, 3)], ssem.at[arr, ph])
    greet(credit, core, coords)
    wait_bytes(zbuf, xssem)
    for s in range(NG):
        for t in range(NT):
            arrived(0, s, t, 2)

    def tphase(s, q, ph):
        dim = (s + q + ph) % 3
        src = (sb, r1b, r2b)[ph]
        dst = (r1b, r2b, sa)[ph]

        def at(p):
            return (s,) + p + (full, qcols(q))

        def final(p):
            return (tile[s],) + p + (full, qcols(q))
        dst_at = final if ph == 2 else at
        send_phase(core, coords, dim, lambda p: src.at[at(p)], lambda p: dst.at[dst_at(p)], tssem.at[ph], trsem.at[s, q, ph])
        keep_own(coords, dim, src, at, dst, dst_at)

    def tarrived(s, q, ph):
        wait_bytes(r1b.at[s, pl.ds(0, 3), full, full, full, qcols(q)], trsem.at[s, q, ph])

    for s in range(NG):
        for t in range(NT):
            arrived(1, s, t, 2)
        for q in range(NQ):
            acc = lax.dot_general(aa[s].reshape(CH * TR, N), bb[q].reshape(KQ, N), (((1,), (1,)), ((), ())),
                                  preferred_element_type=F32)
            sb[s, :, :, :, :, qcols(q)] = acc.astype(BF).reshape(SIDE, SIDE, SIDE, TR, KQ)
            if s == 0 and q == 0:
                pl.semaphore_wait(credit, GREETED)
            tphase(s, q, 0)
    for ph in (1, 2):
        for q in range(NQ):
            for s in range(NG):
                tarrived(s, q, ph - 1)
                tphase(s, q, ph)

    def swap(q):
        return pltpu.make_async_remote_copy(
            src_ref=sa.at[pl.ds(1 - core, 2), :, :, :, :, qcols(q)], dst_ref=r1a.at[pl.ds(0, 2), :, :, :, :, qcols(q)],
            send_sem=dssem.at[q], recv_sem=drsem.at[q], device_id=partner, device_id_type=MESH)

    def store(q):
        return pltpu.make_async_copy(obuf.at[q % 2], out_hbm.at[:, qcols(q), :], osem.at[q])

    def finish(q):
        def own(i):
            return sa[pl.ds(core, 2), i // SIDE, i % SIDE, :, :, qcols(q)].astype(F32)

        def par(i):
            return r1a[pl.ds(0, 2), i // SIDE, i % SIDE, :, :, qcols(q)].astype(F32)

        def add(i, acc):
            return acc + jnp.sum(own(i), axis=1) + jnp.sum(par(i), axis=1)
        zero = jnp.zeros((2, TR, KQ), F32)
        mean = lax.fori_loop(0, SIDE * SIDE, add, zero) * (1.0 / C)

        def add_sq(i, acc):
            u, v = own(i) - mean[:, None], par(i) - mean[:, None]
            return acc + jnp.sum(u * u, axis=1) + jnp.sum(v * v, axis=1)
        var = lax.fori_loop(0, SIDE * SIDE, add_sq, zero) * (1.0 / C)
        rstd = lax.rsqrt(var + LN_EPS)

        def spread(i, carry):
            for first, vals in ((core * CH, own(i)), ((1 - core) * CH, par(i))):
                for k in range(SIDE):
                    c = first + i * SIDE + k
                    v = (vals[:, k] - mean) * rstd * hid_ref[0, c] + hid_ref[1, c]
                    for b in range(2):
                        for lt in range(KQ // 128):
                            y[lt, pl.ds(b * TR * YSK + c, TR, stride=YSK), :] = v[b, :, lt * 128:(lt + 1) * 128]
            return carry
        lax.fori_loop(0, SIDE * SIDE, spread, 0)

        def row(r, carry):
            at = pl.ds((r + 4 * core) * YSK, C)
            yt = jnp.concatenate([y[lt, at, :] for lt in range(KQ // 128)], axis=1).astype(BF)
            update = lax.dot_general(yt, wo_ref[...], (((0,), (0,)), ((), ())), preferred_element_type=F32)
            gate = sigmoid(jnp.dot(xall[core * RL + r, qcols(q), :], wg_ref[...], preferred_element_type=F32))
            obuf[q % 2, r] = (zbuf[r, qcols(q), :].astype(F32) + gate * update).astype(BF)
            return carry
        lax.fori_loop(0, RL, row, 0, unroll=2)

    def ready(q):
        for s in range(NG):
            tarrived(s, q, 2)
        swap(q).start()

    ready(0)
    for q in range(NQ):
        if q + 1 < NQ:
            ready(q + 1)
        swap(q).wait_recv()
        if q >= 2:
            store(q - 2).wait()
        finish(q)
        store(q).start()
    for q in range(NQ):
        swap(q).wait_send()
    for ph in range(3):
        wait_bytes(r1a.at[:, pl.ds(0, 3)], tssem.at[ph])
    wait_bytes(r1a.at[:, pl.ds(0, 3)], ssem.at[1, 2])
    store(NQ - 2).wait()
    store(NQ - 1).wait()


def solution(mesh):
    row_spec = P(('data', 'dap'), None, None)
    mask_spec = P(('data', 'dap'), None)
    replicated = P()
    vspec = pl.BlockSpec(memory_space=VMEM)
    aspec = pl.BlockSpec(memory_space=ANY)

    def local_fn(z_loc, mask_loc, ln_scale, ln_bias, w_a, w_a_gate, w_b, w_b_gate, w_gate, ln_hid_scale, ln_hid_bias, w_out):
        sets = VMEM((NG, SIDE, SIDE, SIDE, TR, N), BF)
        hid = jnp.stack([ln_hid_scale, ln_hid_bias]).astype(F32)
        return pl.pallas_call(
            update_kernel, name='update',
            out_shape=jax.ShapeDtypeStruct((RL, N, C), BF),
            in_specs=[pl.BlockSpec(memory_space=pltpu.SMEM), aspec] + [vspec] * 9, out_specs=aspec,
            scratch_shapes=[
                VMEM((RL, N, C), BF), VMEM((2 * RL, N, C), BF), VMEM((2, RL, N), jnp.int32), VMEM((4, C, C), BF),
                VMEM((KT // 128, CH * SKEW, 128), F32), VMEM((KT // 128, CH * SKEW, 128), F32),
                sets, sets, sets, sets, sets, sets, sets, VMEM((SIDE, SIDE, SIDE, NG, TR, N), BF),
                VMEM((KQ // 128, 2 * TR * YSK, 128), F32), VMEM((2, RL, KQ, C), BF),
                DMA((NT + 1,)), DMA, DMA((NT,)), DMA((NT,)), DMA, DMA, DMA((2, 3)), DMA((2, NG, NT, 3)),
                DMA((3,)), DMA((NG, NQ, 3)), DMA((NQ,)), DMA((NQ,)), DMA((NQ,)), pltpu.SemaphoreType.REGULAR],
            compiler_params=pltpu.CompilerParams(collective_id=1, has_side_effects=True, vmem_limit_bytes=67043328),
        )(hid, z_loc, mask_loc, ln_scale.reshape(1, C), ln_bias.reshape(1, C), w_a, w_a_gate, w_b, w_b_gate, w_gate, w_out)

    return jax.shard_map(local_fn, mesh=mesh, in_specs=(row_spec, mask_spec) + (replicated,) * 10, out_specs=row_spec, check_vma=False)
```

time: 543 us -> 197 us (0.36); the launches traced: 533 us -> 196 us
  waiting for transfers between devices: 213 us -> 0 us
  Pallas kernels: 0 us -> 190 us
  local copies, waits for them, and re-layouts: 127 us -> 4.83 us
  other arithmetic: 108 us -> 1.24 us
  matrix products: 50.7 us -> 0 us
  starting transfers between devices: 33.5 us -> 0 us
    all_to_all x3 -> x0, waiting for transfers between devices: 213 us -> none  [the longest x1 82.3 us: local_fn(): a_chan = lax.all_to_all(a_side, 'dap', 0, 1, tiled=True)]
    pallas_call x0 -> x1, Pallas kernels: none -> 190 us  [local_fn(): pl.pallas_call(update_kernel, name='update', out_shape=jax.ShapeDtypeStru...]
    convert_element_type x4 -> x0, local copies, waits for them, and re-layouts: 76.5 us -> none  [the longest x1 52.2 us: local_fn(): jnp.einsum('cik,cjk->cij', a_chan, b_chan, preferred_element_type=jnp.flo...]
    convert_element_type x8 -> x1, other arithmetic: 53.9 us -> 1.24 us  [local_fn(): hid = jnp.stack([ln_hid_scale, ln_hid_bias]).astype(F32)]
    dot_general x4 -> x0, matrix products: 50.7 us -> none  [the longest x1 15.4 us: gated_pair(): jnp.einsum('rkd,de->erk', x_norm, w_cat, preferred_element_type=jnp.float32)]
    all_to_all x3 -> x0, starting transfers between devices: 33.5 us -> none  [the longest x1 14.1 us: local_fn(): tri_rows = lax.all_to_all(tri_chan, 'dap', 1, 0, tiled=True)]
    unnamed x2 -> x0, other arithmetic: 31.8 us -> none
    unnamed x35 -> x1, local copies, waits for them, and re-layouts: 34 us -> 4.83 us
  transfers between devices with their start and end apart: 3 -> 0, of which waited for: 3 -> 0; matrix products, arithmetic and copies ran while one was open for 5% -> 0% of each run, Pallas kernels for 0% -> 0%
where the time goes in v2:
time: 197 us; the launch traced here: 196 us
  Pallas kernels  190 us (96%)
  local copies, waits for them, and re-layouts  4.83 us (2%)
    pallas_call x1, Pallas kernels, local_fn(): pl.pallas_call(update_kernel, name='update', out_shape=jax.ShapeDtypeStru...  190 us
    unnamed x1, local copies, waits for them, and re-layouts  4.83 us

profile of v2, /device:TPU:1, one launch (start us, length us, event | category | flops | bytes accessed | tf_op | source)
XLA Modules:
  0.0 196.5 jit_solution(13168765206273976111)
XLA Ops:
  0.0 1.2 maximum_convert_fusion.hid_ref
  1.2 190.4 %update.1 = bf16[12,1536,128]{2,1,0:T(8,128)(2,1)} custom-call(f32[2,128]{1,0:T(2,128)} %maximum_convert_fusion.hid_ref, bf16[12,1536,128]{2,1,0:T(8,128)(2,1)} %z_hbm.1, s32[12,1536]{1,0:T(8,128)} %mask_ref.1, bf16[1,128]{1,0:T(2,128)(2,1)} %bitcast.6, bf16[1,128]{1,0:T(2,128)(2,1)} %bitcast.7, bf16[128,128]{1,0:T(8,128)(2,1)} %wa_ref.1, ...), custom_call_target="tpu_custom_call" | custom-call | tf_op jit(solution)/shard_map/update/pallas_call | solution.py:332
  191.6 4.8 %copy.14 = bf16[12,1536,128]{2,1,0:T(8,128)(2,1)} copy(bf16[12,1536,128]{2,1,0:T(8,128)(2,1)} %update.1) | data formatting | bytes 9437184

commit v3 on v2

v3 whole, which is shorter than its diff:
```python
import functools

import jax
import jax.numpy as jnp
from jax import lax
from jax.experimental import pallas as pl
from jax.experimental.pallas import tpu as pltpu
from jax.sharding import PartitionSpec as P

LN_EPS = 1e-5
MESH = pl.DeviceIdType.MESH
DMA = pltpu.SemaphoreType.DMA
VMEM = pltpu.VMEM
ANY = pl.ANY
N = 1536
C = 128
SIDE = 4
CH = 64
RL = 12
TR = 8
NG = 3
KC = 256
PARTS = ((0, 256), (2, 512), (1, 512))
UNITS = [(s, at, width) for s, width in PARTS for at in range(0, N, width)]
KT = 512
NQ = 6
KQ = N // NQ
SKEW = 9
YSK = 129
BF = jnp.bfloat16
F32 = jnp.float32


def place():
    me = lax.axis_index('dap')
    chip, core = me // 2, me % 2
    return core, (chip // 16, (chip // 4) % 4, chip % 4)


def dev(coords, core):
    return {'dap': (coords[0] * 16 + coords[1] * 4 + coords[2]) * 2 + core}


def shift(coords, dim, by):
    return tuple((v + by) % SIDE if i == dim else v for i, v in enumerate(coords))


def pick(dim, at):
    return tuple(at if i == dim else slice(None) for i in range(3))


def greet(sem, core, coords):
    for dim in range(3):
        for by in range(1, SIDE):
            pl.semaphore_signal(sem, inc=1, device_id=dev(shift(coords, dim, by), core), device_id_type=MESH)
    pl.semaphore_signal(sem, inc=1, device_id=dev(coords, 1 - core), device_id_type=MESH)


GREETED = 3 * (SIDE - 1) + 1


def wait_bytes(ref, sem):
    pltpu.make_async_copy(ref, ref, sem).wait()


def send_phase(ring, coords, dim, src_at, dst_at, ssem, rsem):
    for to, device in ring[dim]:
        pltpu.make_async_remote_copy(
            src_ref=src_at(pick(dim, to)), dst_ref=dst_at(pick(dim, coords[dim])), send_sem=ssem, recv_sem=rsem,
            device_id=device, device_id_type=MESH).start()


def loop(steps, body, unroll=None):
    def step(i, carry):
        body(i)
        return carry
    lax.fori_loop(0, steps, step, 0, unroll=unroll)


def keep_own(coords, dim, src, src_at, dst, dst_at):
    own = pick(dim, coords[dim])
    dst[dst_at(own)] = src[src_at(own)]


def sigmoid(v):
    return 0.5 * jnp.tanh(0.5 * v) + 0.5


def update_kernel(z_hbm, mask_ref, scale_ref, bias_ref, wa_ref, wag_ref, wb_ref, wbg_ref, wg_ref, wo_ref, hs_ref, hb_ref, out_hbm,
                  zbuf, xall, mall, wt, stage_a, stage_b, sa, sb, r1a, r1b, r2a, r2b, aa, bb, y, obuf, hid,
                  zsem, xssem, xown, xmix, mrsem, msem, ssem, rsem, tssem, trsem, dssem, drsem, osem, credit):
    core, coords = place()
    barrier = pltpu.get_barrier_semaphore()
    greet(barrier, core, coords)
    partner = dev(coords, 1 - core)
    ring = [[((coords[d] + by) % SIDE, dev(shift(coords, d, by), core)) for by in (1, 3, 2)] for d in range(3)]
    own0, mix0 = 4 * core, 8 - 8 * core
    tile = [s + core * (2 - 2 * s) for s in range(NG)]
    full = slice(None)

    def qcols(q):
        return pl.ds(q * KQ, KQ)

    first = [u for u in UNITS if u[0] == 0]
    loads = [pltpu.make_async_copy(z_hbm.at[pl.ds(own0, TR), pl.ds(at, w)], zbuf.at[pl.ds(own0, TR), pl.ds(at, w)], zsem.at[n])
             for n, (_, at, w) in enumerate(first)]
    loads.append(pltpu.make_async_copy(z_hbm.at[pl.ds(mix0, 4)], zbuf.at[pl.ds(mix0, 4)], zsem.at[len(first)]))
    for cp in loads:
        cp.start()
    for i, w in enumerate((wa_ref, wag_ref, wb_ref, wbg_ref)):
        wt[i] = w[...].astype(F32).T.astype(BF)
    mall[core] = mask_ref[...]
    for i, h in enumerate((hs_ref, hb_ref)):
        hid[i] = jnp.broadcast_to(h[...].astype(F32), (C, C)).T
    scale = scale_ref[...].astype(F32)
    bias = bias_ref[...].astype(F32)
    half = pl.ds(pl.multiple_of(core * CH, CH), CH)
    wcat = jnp.concatenate([wt[i, half, :] for i in range(4)], axis=0)

    def norm(row0, rows, start, width):
        def body(i, carry):
            r = row0 + i
            for k in range(width // KC):
                at = pl.ds(start + k * KC, KC)
                v = zbuf[r, at, :].astype(F32)
                centered = v - jnp.mean(v, axis=-1, keepdims=True)
                var = jnp.mean(centered * centered, axis=-1, keepdims=True)
                xall[core * RL + r, at, :] = (centered * lax.rsqrt(var + LN_EPS) * scale + bias).astype(BF)
            return carry
        lax.fori_loop(0, rows, body, 0, unroll=2)

    def give_x(row0, rows, start, width, sem):
        block = xall.at[pl.ds(core * RL + row0, rows), pl.ds(start, width)]
        pltpu.make_async_remote_copy(src_ref=block, dst_ref=block, send_sem=xssem, recv_sem=sem,
                                     device_id=partner, device_id_type=MESH).start()

    bufs = ((sb, r1b, r2b), (sa, r1a, r2a))

    def phase(arr, n, ph):
        s, start, width = UNITS[n]
        cols = pl.ds(start, width)
        dim = (n + ph) % 3
        src = bufs[arr][ph]

        def at(p):
            return (s,) + p + (full, cols)

        def final(p):
            return p + (tile[s], full, cols) if arr == 0 else at(p)
        dst = (bb, aa)[arr] if ph == 2 else bufs[arr][ph + 1]
        dst_at = final if ph == 2 else at
        send_phase(ring, coords, dim, lambda p: src.at[at(p)], lambda p: dst.at[dst_at(p)], ssem.at[arr, ph],
                   rsem.at[arr, n, ph])
        keep_own(coords, dim, src, at, dst, dst_at)

    def arrived(arr, n, ph):
        s, start, width = UNITS[n]
        wait_bytes(r1a.at[s, pl.ds(0, 3), full, full, full, pl.ds(start, width)], rsem.at[arr, n, ph])

    def make_unit(n):
        s, start, width = UNITS[n]

        def project_row(i, carry):
            row = tile[s] * TR + i
            owner, within = row // RL, row % RL
            for j in range(width // KC):
                at = pl.ds(start + j * KC, KC)
                p = lax.dot_general(wcat, xall[row, at, :], (((1,), (1,)), ((), ())), preferred_element_type=F32)
                keep = mall[owner, pl.ds(within, 1), at].astype(F32)
                a = sigmoid(p[CH:2 * CH]) * p[:CH] * keep
                b = sigmoid(p[3 * CH:]) * p[2 * CH:3 * CH] * keep
                for u in range(KC // 128):
                    lanes = slice(u * 128, (u + 1) * 128)
                    kt = j * (KC // 128) + u
                    stage_a[kt, pl.ds(i, CH, stride=SKEW), :] = a[:, lanes]
                    stage_b[kt, pl.ds(i, CH, stride=SKEW), :] = b[:, lanes]
            return carry
        lax.fori_loop(0, TR, project_row, 0, unroll=4)
        for arr, stage in ((0, stage_b), (1, stage_a)):
            s_ref = bufs[arr][0]

            def pack(i):
                def pack_y(k):
                    def pack_x(m):
                        c = (i * SIDE + k) * SIDE + m
                        for j in range(width // KC):
                            v = jnp.concatenate([stage[2 * j + u, pl.ds(c * SKEW, TR), :] for u in range(2)], axis=1)
                            s_ref[s, i, k, m, :, pl.ds(start + j * KC, KC)] = v.astype(BF)
                    loop(SIDE, pack_x, unroll=SIDE)
                loop(SIDE, pack_y)
            loop(SIDE, pack)
            phase(arr, n, 0)

    def forward(arr, n, ph):
        arrived(arr, n, ph - 1)
        phase(arr, n, ph)

    for n, (s, start, width) in enumerate(UNITS):
        if s == 0:
            loads[n].wait()
            norm(own0, TR, start, width)
            if n == 0:
                pl.semaphore_wait(barrier, GREETED)
                mcopy = pltpu.make_async_remote_copy(src_ref=mask_ref, dst_ref=mall.at[core], send_sem=msem, recv_sem=mrsem,
                                                     device_id=partner, device_id_type=MESH)
                mcopy.start()
            give_x(own0, TR, start, width, xown.at[n])
        if n == len(first):
            mcopy.wait()
            for k, (_, at, w) in enumerate(first):
                wait_bytes(xall.at[pl.ds(0, TR), pl.ds(at, w)], xown.at[k])
        if n == len(first) + 1:
            loads[len(first)].wait()
            norm(mix0, 4, 0, N)
            give_x(mix0, 4, 0, N, xmix)
        if s == 1 and start == 0:
            wait_bytes(xall.at[pl.ds(0, 4)], xmix)
        make_unit(n)

    for n in range(len(UNITS)):
        forward(0, n, 1)
        forward(1, n, 1)
    for arr in range(2):
        for n in range(len(UNITS)):
            forward(arr, n, 2)
    for arr, ph in ((0, 0), (1, 0), (0, 1), (1, 1), (0, 2)):
        wait_bytes(r1a.at[:, pl.ds(0, 3)], ssem.at[arr, ph])
    greet(credit, core, coords)
    wait_bytes(zbuf, xssem)
    for n in range(len(UNITS)):
        arrived(0, n, 2)

    def tphase(s, q, ph):
        dim = (s + q + ph) % 3
        src = (sb, r1b, r2b)[ph]
        dst = (r1b, r2b, sa)[ph]

        def at(p):
            return (s,) + p + (full, qcols(q))

        def final(p):
            return (tile[s],) + p + (full, qcols(q))
        dst_at = final if ph == 2 else at
        send_phase(ring, coords, dim, lambda p: src.at[at(p)], lambda p: dst.at[dst_at(p)], tssem.at[ph], trsem.at[s, q, ph])
        keep_own(coords, dim, src, at, dst, dst_at)

    def tarrived(s, q, ph):
        wait_bytes(r1b.at[s, pl.ds(0, 3), full, full, full, qcols(q)], trsem.at[s, q, ph])

    order = [s for s, _ in PARTS]
    slab = N // SIDE
    for s in order:
        for n, unit in enumerate(UNITS):
            if unit[0] == s:
                arrived(1, n, 2)
        for k in range(SIDE):
            acc = lax.dot_general(aa[s].reshape(CH * TR, N), bb[k].reshape(slab, N), (((1,), (1,)), ((), ())),
                                  preferred_element_type=F32)
            sb[s, :, :, :, :, pl.ds(k * slab, slab)] = acc.astype(BF).reshape(SIDE, SIDE, SIDE, TR, slab)
            if s == order[0] and k == 0:
                pl.semaphore_wait(credit, GREETED)
            for q in range(NQ):
                if k * slab < (q + 1) * KQ <= (k + 1) * slab:
                    tphase(s, q, 0)
    for ph in (1, 2):
        for q in range(NQ):
            for s in order:
                tarrived(s, q, ph - 1)
                tphase(s, q, ph)

    def swap(q):
        return pltpu.make_async_remote_copy(
            src_ref=sa.at[pl.ds(1 - core, 2), :, :, :, :, qcols(q)], dst_ref=r1a.at[pl.ds(0, 2), :, :, :, :, qcols(q)],
            send_sem=dssem.at[q], recv_sem=drsem.at[q], device_id=partner, device_id_type=MESH)

    def store(q):
        return pltpu.make_async_copy(obuf.at[q % 2], out_hbm.at[:, qcols(q), :], osem.at[q])

    def finish(q):
        def own(i):
            return sa[pl.ds(core, 2), i // SIDE, i % SIDE, :, :, qcols(q)].astype(F32)

        def par(i):
            return r1a[pl.ds(0, 2), i // SIDE, i % SIDE, :, :, qcols(q)].astype(F32)

        def add(i, acc):
            return acc + jnp.sum(own(i), axis=1) + jnp.sum(par(i), axis=1)
        zero = jnp.zeros((2, TR, KQ), F32)
        mean = lax.fori_loop(0, SIDE * SIDE, add, zero) * (1.0 / C)

        def add_sq(i, acc):
            u, v = own(i) - mean[:, None], par(i) - mean[:, None]
            return acc + jnp.sum(u * u, axis=1) + jnp.sum(v * v, axis=1)
        var = lax.fori_loop(0, SIDE * SIDE, add_sq, zero) * (1.0 / C)
        rstd = lax.rsqrt(var + LN_EPS)

        def spread(i, carry):
            for first, vals in ((core * CH, own(i)), ((1 - core) * CH, par(i))):
                for k in range(SIDE):
                    c = first + i * SIDE + k
                    v = (vals[:, k] - mean) * rstd
                    for b in range(2):
                        for lt in range(KQ // 128):
                            y[lt, pl.ds(b * TR * YSK + c, TR, stride=YSK), :] = v[b, :, lt * 128:(lt + 1) * 128]
            return carry
        lax.fori_loop(0, SIDE * SIDE, spread, 0)
        if q + 1 < NQ:
            ready(q + 1)

        def row(r, carry):
            at = pl.ds((r + 4 * core) * YSK, C)
            yt = jnp.concatenate([y[lt, at, :] * hid[0] + hid[1] for lt in range(KQ // 128)], axis=1).astype(BF)
            update = lax.dot_general(yt, wo_ref[...], (((0,), (0,)), ((), ())), preferred_element_type=F32)
            gate = sigmoid(jnp.dot(xall[core * RL + r, qcols(q), :], wg_ref[...], preferred_element_type=F32))
            obuf[q % 2, r] = (zbuf[r, qcols(q), :].astype(F32) + gate * update).astype(BF)
            return carry
        lax.fori_loop(0, RL, row, 0, unroll=3)

    def ready(q):
        for s in range(NG):
            tarrived(s, q, 2)
        swap(q).start()

    ready(0)
    for q in range(NQ):
        swap(q).wait_recv()
        if q >= 2:
            store(q - 2).wait()
        finish(q)
        store(q).start()
    for q in range(NQ):
        swap(q).wait_send()
    for ph in range(3):
        wait_bytes(r1a.at[:, pl.ds(0, 3)], tssem.at[ph])
    wait_bytes(r1a.at[:, pl.ds(0, 3)], ssem.at[1, 2])
    store(NQ - 2).wait()
    store(NQ - 1).wait()


def solution(mesh):
    row_spec = P(('data', 'dap'), None, None)
    mask_spec = P(('data', 'dap'), None)
    replicated = P()
    vspec = pl.BlockSpec(memory_space=VMEM)
    aspec = pl.BlockSpec(memory_space=ANY)

    def local_fn(z_loc, mask_loc, ln_scale, ln_bias, w_a, w_a_gate, w_b, w_b_gate, w_gate, ln_hid_scale, ln_hid_bias, w_out):
        sets = VMEM((NG, SIDE, SIDE, SIDE, TR, N), BF)
        return pl.pallas_call(
            update_kernel, name='update',
            out_shape=jax.ShapeDtypeStruct((RL, N, C), BF),
            in_specs=[aspec] + [vspec] * 11, out_specs=aspec,
            scratch_shapes=[
                VMEM((RL, N, C), BF), VMEM((2 * RL, N, C), BF), VMEM((2, RL, N), jnp.int32), VMEM((4, C, C), BF),
                VMEM((KT // 128, CH * SKEW, 128), F32), VMEM((KT // 128, CH * SKEW, 128), F32),
                sets, sets, sets, sets, sets, sets, sets, VMEM((SIDE, SIDE, SIDE, NG, TR, N), BF),
                VMEM((KQ // 128, 2 * TR * YSK, 128), F32), VMEM((2, RL, KQ, C), BF), VMEM((2, C, C), F32),
                DMA((len(UNITS),)), DMA, DMA((len(UNITS),)), DMA, DMA, DMA, DMA((2, 3)), DMA((2, len(UNITS), 3)),
                DMA((3,)), DMA((NG, NQ, 3)), DMA((NQ,)), DMA((NQ,)), DMA((NQ,)), pltpu.SemaphoreType.REGULAR],
            compiler_params=pltpu.CompilerParams(collective_id=1, has_side_effects=True, vmem_limit_bytes=67043328),
        )(z_loc, mask_loc, ln_scale.reshape(1, C), ln_bias.reshape(1, C), w_a, w_a_gate, w_b, w_b_gate, w_gate, w_out,
          ln_hid_scale.reshape(1, C), ln_hid_bias.reshape(1, C))

    return jax.shard_map(local_fn, mesh=mesh, in_specs=(row_spec, mask_spec) + (replicated,) * 10, out_specs=row_spec, check_vma=False)
```

time: 197 us -> 180 us (0.914)
  Pallas kernels: 190 us -> 175 us
    pallas_call x1, Pallas kernels: 190 us -> 175 us  [local_fn(): pl.pallas_call(update_kernel, name='update', out_shape=jax.ShapeDtypeStru...]
where the time goes in v3:
time: 180 us
  Pallas kernels  175 us (97%)
  local copies, waits for them, and re-layouts  4.83 us (3%)
    pallas_call x1, Pallas kernels, local_fn(): pl.pallas_call(update_kernel, name='update', out_shape=jax.ShapeDtypeStru...  175 us
    unnamed x1, local copies, waits for them, and re-layouts  4.83 us

profile of v3, /device:TPU:1, one launch (start us, length us, event | category | flops | bytes accessed | tf_op | source)
XLA Modules:
  0.0 180.1 jit_solution(14355155104509567033)
XLA Ops:
  0.0 175.3 %update.1 = bf16[12,1536,128]{2,1,0:T(8,128)(2,1)} custom-call(bf16[12,1536,128]{2,1,0:T(8,128)(2,1)} %z_hbm.1, s32[12,1536]{1,0:T(8,128)} %mask_ref.1, bf16[1,128]{1,0:T(2,128)(2,1)} %bitcast.4, bf16[1,128]{1,0:T(2,128)(2,1)} %bitcast.5, bf16[128,128]{1,0:T(8,128)(2,1)} %wa_ref.1, bf16[128,128]{1,0:T(8,128)(2,1)} %wag_ref.1, bf16[128,128]{1,0:T(8,128)(2,1)} %wb_ref.1, ...), custom_call_target="tpu_custom_call" | custom-call | tf_op jit(solution)/shard_map/update/pallas_call | solution.py:349
  175.3 4.8 %copy.14 = bf16[12,1536,128]{2,1,0:T(8,128)(2,1)} copy(bf16[12,1536,128]{2,1,0:T(8,128)(2,1)} %update.1) | data formatting | bytes 9437184

commit v4 on v3

--- a/solution.py
+++ b/solution.py
@@ -27,6 +27,7 @@
 KQ = N // NQ
 SKEW = 9
 YSK = 129
+PASS = 4
 BF = jnp.bfloat16
 F32 = jnp.float32
 
@@ -86,9 +87,87 @@
     return 0.5 * jnp.tanh(0.5 * v) + 0.5
 
 
-def update_kernel(z_hbm, mask_ref, scale_ref, bias_ref, wa_ref, wag_ref, wb_ref, wbg_ref, wg_ref, wo_ref, hs_ref, hb_ref, out_hbm,
+def hidden_norm(core, own, par, y, midway):
+    def add(i, acc):
+        return acc + jnp.sum(own(i), axis=1) + jnp.sum(par(i), axis=1)
+    zero = jnp.zeros((2, TR, KQ), F32)
+    mean = lax.fori_loop(0, SIDE * SIDE, add, zero) * (1.0 / C)
+
+    def add_sq(i, acc):
+        u, v = own(i) - mean[:, None], par(i) - mean[:, None]
+        return acc + jnp.sum(u * u, axis=1) + jnp.sum(v * v, axis=1)
+    var = lax.fori_loop(0, SIDE * SIDE, add_sq, zero) * (1.0 / C)
+    rstd = lax.rsqrt(var + LN_EPS)
+    midway()
+
+    def spread(i):
+        for first, vals in ((core * CH, own(i)), ((1 - core) * CH, par(i))):
+            for k in range(SIDE):
+                c = first + i * SIDE + k
+                v = (vals[:, k] - mean) * rstd
+                for b in range(2):
+                    for lt in range(KQ // 128):
+                        y[lt, pl.ds(b * TR * YSK + c, TR, stride=YSK), :] = v[b, :, lt * 128:(lt + 1) * 128]
+    loop(SIDE * SIDE, spread)
+
+
+def out_rows(core, y, hid, wo_ref, wg_ref, x_at, put, first=0, count=RL):
+    def row(i):
+        r = first + i
+        at = pl.ds((r + 4 * core) * YSK, C)
+        yt = jnp.concatenate([y[lt, at, :] * hid[0] + hid[1] for lt in range(KQ // 128)], axis=1).astype(BF)
+        update = lax.dot_general(yt, wo_ref[...], (((0,), (0,)), ((), ())), preferred_element_type=F32)
+        put(r, sigmoid(jnp.dot(x_at(r), wg_ref[...], preferred_element_type=F32)) * update)
+    loop(count, row, unroll=3)
+
+
+def set_hidden(hid, hs_ref, hb_ref):
+    for i, h in enumerate((hs_ref, hb_ref)):
+        hid[i] = jnp.broadcast_to(h[...].astype(F32), (C, C)).T
+
+
+def last_kernel(part, own_hbm, par_hbm, x_hbm, z_hbm, wg_hbm, wo_hbm, hs_hbm, hb_hbm, out_hbm,
+                keep, own_v, par_v, xv, zv, wg_ref, wo_ref, hs_ref, hb_ref, ov, y, hid, isem, ksem, osem):
+    core = lax.axis_index('dap') % 2
+    done = N - KQ
+    cols = pl.ds(done, KQ)
+    pairs = ((hs_hbm, hs_ref), (hb_hbm, hb_ref), (own_hbm, own_v), (par_hbm, par_v), (wg_hbm, wg_ref), (wo_hbm, wo_ref),
+             (x_hbm, xv), (z_hbm.at[:, cols, :], zv))
+    loads = [pltpu.make_async_copy(a, b, isem.at[n]) for n, (a, b) in enumerate(pairs)]
+    some = [pl.ds(r, RL // PASS) for r in range(0, RL, RL // PASS)]
+    ins = [pltpu.make_async_copy(part.at[r, pl.ds(0, done)], keep.at[r], ksem.at[n]) for n, r in enumerate(some)]
+    outs = [pltpu.make_async_copy(keep.at[r], out_hbm.at[r, pl.ds(0, done)], osem.at[n]) for n, r in enumerate(some)]
+    for cp in loads + ins:
+        cp.start()
+    for cp in loads[:4]:
+        cp.wait()
+    set_hidden(hid, hs_ref, hb_ref)
+
+    def midway():
+        for a, b in zip(ins, outs):
+            a.wait()
+            b.start()
+        for cp in loads[4:]:
+            cp.wait()
+
+    def put(r, v):
+        ov[r] = (zv[r].astype(F32) + v).astype(BF)
+    hidden_norm(core, lambda i: own_v[:, i // SIDE, i % SIDE].astype(F32), lambda i: par_v[:, i // SIDE, i % SIDE].astype(F32), y, midway)
+    ends = []
+    for n in range(2):
+        rows = pl.ds(n * RL // 2, RL // 2)
+        out_rows(core, y, hid, wo_ref, wg_ref, lambda r: xv[r], put, n * RL // 2, RL // 2)
+        ends.append(pltpu.make_async_copy(ov.at[rows], out_hbm.at[rows, cols, :], osem.at[PASS + n]))
+        ends[-1].start()
+    for cp in outs + ends:
+        cp.wait()
+
+
+def update_kernel(z_hbm, *refs):
+    small, refs = refs[:11], refs[11:]
+    (out_hbm, own_out, par_out, x_out, mask_ref, scale_ref, bias_ref, wa_ref, wag_ref, wb_ref, wbg_ref, wg_ref, wo_ref, hs_ref, hb_ref,
                   zbuf, xall, mall, wt, stage_a, stage_b, sa, sb, r1a, r1b, r2a, r2b, aa, bb, y, obuf, hid,
-                  zsem, xssem, xown, xmix, mrsem, msem, ssem, rsem, tssem, trsem, dssem, drsem, osem, credit):
+                  zsem, xssem, xown, xmix, mrsem, msem, ssem, rsem, lsem, dssem, drsem, osem, credit, wsem) = refs
     core, coords = place()
     barrier = pltpu.get_barrier_semaphore()
     greet(barrier, core, coords)
@@ -105,29 +184,37 @@
     loads = [pltpu.make_async_copy(z_hbm.at[pl.ds(own0, TR), pl.ds(at, w)], zbuf.at[pl.ds(own0, TR), pl.ds(at, w)], zsem.at[n])
              for n, (_, at, w) in enumerate(first)]
     loads.append(pltpu.make_async_copy(z_hbm.at[pl.ds(mix0, 4)], zbuf.at[pl.ds(mix0, 4)], zsem.at[len(first)]))
-    for cp in loads:
+    held = (mask_ref, scale_ref, bias_ref, wa_ref, wag_ref, wb_ref, wbg_ref, wg_ref, wo_ref, hs_ref, hb_ref)
+    copies = [pltpu.make_async_copy(a, b, wsem.at[n]) for n, (a, b) in enumerate(zip(small, held))]
+    loads[0].start()
+    for cp in copies:
         cp.start()
+    for cp in loads[1:]:
+        cp.start()
+    for cp in copies:
+        cp.wait()
     for i, w in enumerate((wa_ref, wag_ref, wb_ref, wbg_ref)):
         wt[i] = w[...].astype(F32).T.astype(BF)
     mall[core] = mask_ref[...]
-    for i, h in enumerate((hs_ref, hb_ref)):
-        hid[i] = jnp.broadcast_to(h[...].astype(F32), (C, C)).T
+    set_hidden(hid, hs_ref, hb_ref)
     scale = scale_ref[...].astype(F32)
     bias = bias_ref[...].astype(F32)
     half = pl.ds(pl.multiple_of(core * CH, CH), CH)
     wcat = jnp.concatenate([wt[i, half, :] for i in range(4)], axis=0)
+
+    average = jnp.full((C, C), 1.0 / C, BF)
 
     def norm(row0, rows, start, width):
         def body(i, carry):
             r = row0 + i
             for k in range(width // KC):
                 at = pl.ds(start + k * KC, KC)
-                v = zbuf[r, at, :].astype(F32)
-                centered = v - jnp.mean(v, axis=-1, keepdims=True)
+                v = zbuf[r, at, :]
+                centered = v.astype(F32) - jnp.dot(v, average, preferred_element_type=F32)
                 var = jnp.mean(centered * centered, axis=-1, keepdims=True)
                 xall[core * RL + r, at, :] = (centered * lax.rsqrt(var + LN_EPS) * scale + bias).astype(BF)
             return carry
-        lax.fori_loop(0, rows, body, 0, unroll=2)
+        lax.fori_loop(0, rows, body, 0, unroll=4 if width == KC else 1)
 
     def give_x(row0, rows, start, width, sem):
         block = xall.at[pl.ds(core * RL + row0, rows), pl.ds(start, width)]
@@ -135,6 +222,11 @@
                                      device_id=partner, device_id_type=MESH).start()
 
     bufs = ((sb, r1b, r2b), (sa, r1a, r2a))
+
+    def unit_sem(arr, n, ph):
+        if ph < 2:
+            return rsem.at[arr, n, ph]
+        return lsem.at[NG] if arr == 0 else lsem.at[UNITS[n][0]]
 
     def phase(arr, n, ph):
         s, start, width = UNITS[n]
@@ -150,7 +242,7 @@
         dst = (bb, aa)[arr] if ph == 2 else bufs[arr][ph + 1]
         dst_at = final if ph == 2 else at
         send_phase(ring, coords, dim, lambda p: src.at[at(p)], lambda p: dst.at[dst_at(p)], ssem.at[arr, ph],
-                   rsem.at[arr, n, ph])
+                   unit_sem(arr, n, ph))
         keep_own(coords, dim, src, at, dst, dst_at)
 
     def arrived(arr, n, ph):
@@ -225,10 +317,16 @@
             forward(arr, n, 2)
     for arr, ph in ((0, 0), (1, 0), (0, 1), (1, 1), (0, 2)):
         wait_bytes(r1a.at[:, pl.ds(0, 3)], ssem.at[arr, ph])
+    wait_bytes(r1a.at[:, pl.ds(0, 3)], lsem.at[NG])
     greet(credit, core, coords)
     wait_bytes(zbuf, xssem)
-    for n in range(len(UNITS)):
-        arrived(0, n, 2)
+
+    x_copy = pltpu.make_async_copy(xall.at[pl.ds(core * RL, RL), qcols(NQ - 1)], x_out, msem)
+    x_copy.start()
+
+    def part_sem(s, q, ph):
+        k = 2 * NG * NQ + q if ph == 2 else (s * NQ + q) * 2 + ph
+        return rsem.at[k // (2 * len(UNITS)), (k // 2) % len(UNITS), k % 2]
 
     def tphase(s, q, ph):
         dim = (s + q + ph) % 3
@@ -241,18 +339,16 @@
         def final(p):
             return (tile[s],) + p + (full, qcols(q))
         dst_at = final if ph == 2 else at
-        send_phase(ring, coords, dim, lambda p: src.at[at(p)], lambda p: dst.at[dst_at(p)], tssem.at[ph], trsem.at[s, q, ph])
+        send_phase(ring, coords, dim, lambda p: src.at[at(p)], lambda p: dst.at[dst_at(p)], ssem.at[0, ph], part_sem(s, q, ph))
         keep_own(coords, dim, src, at, dst, dst_at)
 
     def tarrived(s, q, ph):
-        wait_bytes(r1b.at[s, pl.ds(0, 3), full, full, full, qcols(q)], trsem.at[s, q, ph])
+        wait_bytes(r1b.at[s, pl.ds(0, 3), full, full, full, qcols(q)], part_sem(s, q, ph))
 
     order = [s for s, _ in PARTS]
     slab = N // SIDE
     for s in order:
-        for n, unit in enumerate(UNITS):
-            if unit[0] == s:
-                arrived(1, n, 2)
+        wait_bytes(r1a.at[s, pl.ds(0, 3)], lsem.at[s])
         for k in range(SIDE):
             acc = lax.dot_general(aa[s].reshape(CH * TR, N), bb[k].reshape(slab, N), (((1,), (1,)), ((), ())),
                                   preferred_element_type=F32)
@@ -270,8 +366,9 @@
 
     def swap(q):
         return pltpu.make_async_remote_copy(
-            src_ref=sa.at[pl.ds(1 - core, 2), :, :, :, :, qcols(q)], dst_ref=r1a.at[pl.ds(0, 2), :, :, :, :, qcols(q)],
-            send_sem=dssem.at[q], recv_sem=drsem.at[q], device_id=partner, device_id_type=MESH)
+            src_ref=sa.at[pl.ds(1 - core, 2), :, :, :, :, qcols(q)],
+            dst_ref=r1a.at[pl.ds(0, 2), :, :, :, :, qcols(q)] if q < NQ - 1 else par_out,
+            send_sem=dssem, recv_sem=drsem.at[q], device_id=partner, device_id_type=MESH)
 
     def store(q):
         return pltpu.make_async_copy(obuf.at[q % 2], out_hbm.at[:, qcols(q), :], osem.at[q])
@@ -283,82 +380,68 @@
         def par(i):
             return r1a[pl.ds(0, 2), i // SIDE, i % SIDE, :, :, qcols(q)].astype(F32)
 
-        def add(i, acc):
-            return acc + jnp.sum(own(i), axis=1) + jnp.sum(par(i), axis=1)
-        zero = jnp.zeros((2, TR, KQ), F32)
-        mean = lax.fori_loop(0, SIDE * SIDE, add, zero) * (1.0 / C)
-
-        def add_sq(i, acc):
-            u, v = own(i) - mean[:, None], par(i) - mean[:, None]
-            return acc + jnp.sum(u * u, axis=1) + jnp.sum(v * v, axis=1)
-        var = lax.fori_loop(0, SIDE * SIDE, add_sq, zero) * (1.0 / C)
-        rstd = lax.rsqrt(var + LN_EPS)
-
-        def spread(i, carry):
-            for first, vals in ((core * CH, own(i)), ((1 - core) * CH, par(i))):
-                for k in range(SIDE):
-                    c = first + i * SIDE + k
-                    v = (vals[:, k] - mean) * rstd
-                    for b in range(2):
-                        for lt in range(KQ // 128):
-                            y[lt, pl.ds(b * TR * YSK + c, TR, stride=YSK), :] = v[b, :, lt * 128:(lt + 1) * 128]
-            return carry
-        lax.fori_loop(0, SIDE * SIDE, spread, 0)
-        if q + 1 < NQ:
-            ready(q + 1)
-
-        def row(r, carry):
-            at = pl.ds((r + 4 * core) * YSK, C)
-            yt = jnp.concatenate([y[lt, at, :] * hid[0] + hid[1] for lt in range(KQ // 128)], axis=1).astype(BF)
-            update = lax.dot_general(yt, wo_ref[...], (((0,), (0,)), ((), ())), preferred_element_type=F32)
-            gate = sigmoid(jnp.dot(xall[core * RL + r, qcols(q), :], wg_ref[...], preferred_element_type=F32))
-            obuf[q % 2, r] = (zbuf[r, qcols(q), :].astype(F32) + gate * update).astype(BF)
-            return carry
-        lax.fori_loop(0, RL, row, 0, unroll=3)
+        def put(r, v):
+            obuf[q % 2, r] = (zbuf[r, qcols(q), :].astype(F32) + v).astype(BF)
+        hidden_norm(core, own, par, y, lambda: ready(q + 1))
+        out_rows(core, y, hid, wo_ref, wg_ref, lambda r: xall[core * RL + r, qcols(q), :], put)
 
     def ready(q):
-        for s in range(NG):
-            tarrived(s, q, 2)
+        wait_bytes(r1b.at[:, pl.ds(0, 3), full, full, full, qcols(q)], part_sem(0, q, 2))
         swap(q).start()
-
+        if q == NQ - 1:
+            own_copy.start()
+
+    own_copy = pltpu.make_async_copy(sa.at[pl.ds(core, 2), :, :, :, :, qcols(NQ - 1)], own_out, osem.at[NQ - 1])
     ready(0)
-    for q in range(NQ):
+    for q in range(NQ - 1):
         swap(q).wait_recv()
         if q >= 2:
             store(q - 2).wait()
         finish(q)
         store(q).start()
-    for q in range(NQ):
-        swap(q).wait_send()
+    wait_bytes(sa.at[pl.ds(0, 2)], dssem)
     for ph in range(3):
-        wait_bytes(r1a.at[:, pl.ds(0, 3)], tssem.at[ph])
+        wait_bytes(r1a.at[:, pl.ds(0, 3)], ssem.at[0, ph])
     wait_bytes(r1a.at[:, pl.ds(0, 3)], ssem.at[1, 2])
+    x_copy.wait()
+    store(NQ - 3).wait()
     store(NQ - 2).wait()
-    store(NQ - 1).wait()
+    own_copy.wait()
+    swap(NQ - 1).wait_recv()
 
 
 def solution(mesh):
     row_spec = P(('data', 'dap'), None, None)
     mask_spec = P(('data', 'dap'), None)
     replicated = P()
-    vspec = pl.BlockSpec(memory_space=VMEM)
     aspec = pl.BlockSpec(memory_space=ANY)
 
     def local_fn(z_loc, mask_loc, ln_scale, ln_bias, w_a, w_a_gate, w_b, w_b_gate, w_gate, ln_hid_scale, ln_hid_bias, w_out):
         sets = VMEM((NG, SIDE, SIDE, SIDE, TR, N), BF)
-        return pl.pallas_call(
+        line, square = VMEM((1, C), BF), VMEM((C, C), BF)
+        edge = jax.ShapeDtypeStruct((2, SIDE, SIDE, SIDE, TR, KQ), BF)
+        hs, hb = ln_hid_scale.reshape(1, C), ln_hid_bias.reshape(1, C)
+        part, own, par, x_last = pl.pallas_call(
             update_kernel, name='update',
-            out_shape=jax.ShapeDtypeStruct((RL, N, C), BF),
-            in_specs=[aspec] + [vspec] * 11, out_specs=aspec,
-            scratch_shapes=[
+            out_shape=(jax.ShapeDtypeStruct((RL, N, C), BF), edge, edge, jax.ShapeDtypeStruct((RL, KQ, C), BF)),
+            in_specs=[aspec] * 12, out_specs=(aspec,) * 4,
+            scratch_shapes=[VMEM((RL, N), jnp.int32), line, line] + [square] * 6 + [line] * 2 + [
                 VMEM((RL, N, C), BF), VMEM((2 * RL, N, C), BF), VMEM((2, RL, N), jnp.int32), VMEM((4, C, C), BF),
                 VMEM((KT // 128, CH * SKEW, 128), F32), VMEM((KT // 128, CH * SKEW, 128), F32),
                 sets, sets, sets, sets, sets, sets, sets, VMEM((SIDE, SIDE, SIDE, NG, TR, N), BF),
                 VMEM((KQ // 128, 2 * TR * YSK, 128), F32), VMEM((2, RL, KQ, C), BF), VMEM((2, C, C), F32),
-                DMA((len(UNITS),)), DMA, DMA((len(UNITS),)), DMA, DMA, DMA, DMA((2, 3)), DMA((2, len(UNITS), 3)),
-                DMA((3,)), DMA((NG, NQ, 3)), DMA((NQ,)), DMA((NQ,)), DMA((NQ,)), pltpu.SemaphoreType.REGULAR],
+                DMA((N // PARTS[0][1] + 1,)), DMA, DMA((N // PARTS[0][1],)), DMA, DMA, DMA, DMA((2, 3)), DMA((2, len(UNITS), 2)),
+                DMA((NG + 1,)), DMA, DMA((NQ,)), DMA((NQ,)), pltpu.SemaphoreType.REGULAR, DMA((11,))],
             compiler_params=pltpu.CompilerParams(collective_id=1, has_side_effects=True, vmem_limit_bytes=67043328),
-        )(z_loc, mask_loc, ln_scale.reshape(1, C), ln_bias.reshape(1, C), w_a, w_a_gate, w_b, w_b_gate, w_gate, w_out,
-          ln_hid_scale.reshape(1, C), ln_hid_bias.reshape(1, C))
+        )(z_loc, mask_loc, ln_scale.reshape(1, C), ln_bias.reshape(1, C), w_a, w_a_gate, w_b, w_b_gate, w_gate, w_out, hs, hb)
+        edge_v = VMEM((2, SIDE, SIDE, SIDE, TR, KQ), BF)
+        block = VMEM((RL, KQ, C), BF)
+        return pl.pallas_call(
+            last_kernel, name='last', out_shape=jax.ShapeDtypeStruct((RL, N, C), BF),
+            in_specs=[aspec] * 9, out_specs=aspec,
+            scratch_shapes=[VMEM((RL, N - KQ, C), BF), edge_v, edge_v, block, block, square, square, line, line, block,
+                            VMEM((KQ // 128, 2 * TR * YSK, 128), F32), VMEM((2, C, C), F32), DMA((8,)), DMA((PASS,)), DMA((PASS + 2,))],
+            compiler_params=pltpu.CompilerParams(vmem_limit_bytes=60 * 2**20),
+        )(part, own, par, x_last, z_loc, w_gate, w_out, hs, hb)
 
     return jax.shard_map(local_fn, mesh=mesh, in_specs=(row_spec, mask_spec) + (replicated,) * 10, out_specs=row_spec, check_vma=False)

time: 180 us -> 174 us (0.967)
  local copies, waits for them, and re-layouts: 4.83 us -> 0 us
    unnamed x1 -> x0, local copies, waits for them, and re-layouts: 4.83 us -> none
    pallas_call x1 -> x2, Pallas kernels: 175 us -> 174 us  [the longest x1 169 us: local_fn(): pl.pallas_call(update_kernel, name='update', out_shape=(jax.ShapeDtypeStr...]
where the time goes in v4:
time: 174 us
  Pallas kernels  174 us (100%)
    pallas_call x1, Pallas kernels, local_fn(): pl.pallas_call(update_kernel, name='update', out_shape=(jax.ShapeDtypeStr...  169 us
    pallas_call x1, Pallas kernels, local_fn(): pl.pallas_call(last_kernel, name='last', out_shape=jax.ShapeDtypeStruct((...  5.48 us

profile of v4, /device:TPU:1, one launch (start us, length us, event | category | flops | bytes accessed | tf_op | source)
XLA Modules:
  0.0 174.2 jit_solution(9750510943128617096)
XLA Ops:
  0.0 168.6 %update.1 = (bf16[12,1536,128]{2,1,0:T(8,128)(2,1)}, bf16[2,4,4,4,8,256]{5,4,3,2,1,0:T(8,128)(2,1)}, bf16[2,4,4,4,8,256]{5,4,3,2,1,0:T(8,128)(2,1)}, bf16[12,256,128]{2,1,0:T(8,128)(2,1)}) custom-call(bf16[12,1536,128]{2,1,0:T(8,128)(2,1)} %z_hbm.3, s32[12,1536]{1,0:T(8,128)} %refs_0_.1, bf16[1,128]{1,0:T(2,128)(2,1)} %bitcast.8, bf16[1,128]{1,0:T(2,128)(2,1)} %bitcast.9, ...), custom_call_target="tpu_custom_call" | custom-call | tf_op jit(solution)/shard_map/update/pallas_call | solution.py:424
  168.6 5.5 %last.1 = bf16[12,1536,128]{2,1,0:T(8,128)(2,1)} custom-call(bf16[12,1536,128]{2,1,0:T(8,128)(2,1)} %get-tuple-element.9.part, bf16[2,4,4,4,8,256]{5,4,3,2,1,0:T(8,128)(2,1)} %get-tuple-element.10.own_hbm, bf16[2,4,4,4,8,256]{5,4,3,2,1,0:T(8,128)(2,1)} %get-tuple-element.11.par_hbm, bf16[12,256,128]{2,1,0:T(8,128)(2,1)} %get-tuple-element.12.x_hbm, ...), custom_call_target="tpu_custom_call" | custom-call | tf_op jit(solution)/shard_map/last/pallas_call | solution.py:439

commit v5 on v4

--- a/solution.py
+++ b/solution.py
@@ -91,12 +91,12 @@
     def add(i, acc):
         return acc + jnp.sum(own(i), axis=1) + jnp.sum(par(i), axis=1)
     zero = jnp.zeros((2, TR, KQ), F32)
-    mean = lax.fori_loop(0, SIDE * SIDE, add, zero) * (1.0 / C)
+    mean = lax.fori_loop(0, SIDE * SIDE, add, zero, unroll=2) * (1.0 / C)
 
     def add_sq(i, acc):
         u, v = own(i) - mean[:, None], par(i) - mean[:, None]
         return acc + jnp.sum(u * u, axis=1) + jnp.sum(v * v, axis=1)
-    var = lax.fori_loop(0, SIDE * SIDE, add_sq, zero) * (1.0 / C)
+    var = lax.fori_loop(0, SIDE * SIDE, add_sq, zero, unroll=2) * (1.0 / C)
     rstd = lax.rsqrt(var + LN_EPS)
     midway()
 
@@ -108,7 +108,7 @@
                 for b in range(2):
                     for lt in range(KQ // 128):
                         y[lt, pl.ds(b * TR * YSK + c, TR, stride=YSK), :] = v[b, :, lt * 128:(lt + 1) * 128]
-    loop(SIDE * SIDE, spread)
+    loop(SIDE * SIDE, spread, unroll=2)
 
 
 def out_rows(core, y, hid, wo_ref, wg_ref, x_at, put, first=0, count=RL):
@@ -118,7 +118,7 @@
         yt = jnp.concatenate([y[lt, at, :] * hid[0] + hid[1] for lt in range(KQ // 128)], axis=1).astype(BF)
         update = lax.dot_general(yt, wo_ref[...], (((0,), (0,)), ((), ())), preferred_element_type=F32)
         put(r, sigmoid(jnp.dot(x_at(r), wg_ref[...], preferred_element_type=F32)) * update)
-    loop(count, row, unroll=3)
+    loop(count, row, unroll=6)
 
 
 def set_hidden(hid, hs_ref, hb_ref):
@@ -143,22 +143,21 @@
         cp.wait()
     set_hidden(hid, hs_ref, hb_ref)
 
-    def midway():
-        for a, b in zip(ins, outs):
-            a.wait()
-            b.start()
-        for cp in loads[4:]:
-            cp.wait()
-
     def put(r, v):
         ov[r] = (zv[r].astype(F32) + v).astype(BF)
-    hidden_norm(core, lambda i: own_v[:, i // SIDE, i % SIDE].astype(F32), lambda i: par_v[:, i // SIDE, i % SIDE].astype(F32), y, midway)
+    hidden_norm(core, lambda i: own_v[:, i // SIDE, i % SIDE].astype(F32), lambda i: par_v[:, i // SIDE, i % SIDE].astype(F32), y, lambda: None)
+    for cp in loads[4:]:
+        cp.wait()
     ends = []
     for n in range(2):
         rows = pl.ds(n * RL // 2, RL // 2)
         out_rows(core, y, hid, wo_ref, wg_ref, lambda r: xv[r], put, n * RL // 2, RL // 2)
         ends.append(pltpu.make_async_copy(ov.at[rows], out_hbm.at[rows, cols, :], osem.at[PASS + n]))
         ends[-1].start()
+        if n == 0:
+            for a, b in zip(ins, outs):
+                a.wait()
+                b.start()
     for cp in outs + ends:
         cp.wait()
 
@@ -189,10 +188,10 @@
     loads[0].start()
     for cp in copies:
         cp.start()
+    for cp in copies:
+        cp.wait()
     for cp in loads[1:]:
         cp.start()
-    for cp in copies:
-        cp.wait()
     for i, w in enumerate((wa_ref, wag_ref, wb_ref, wbg_ref)):
         wt[i] = w[...].astype(F32).T.astype(BF)
     mall[core] = mask_ref[...]
@@ -231,7 +230,7 @@
     def phase(arr, n, ph):
         s, start, width = UNITS[n]
         cols = pl.ds(start, width)
-        dim = (n + ph) % 3
+        dim = (n + arr + ph) % 3
         src = bufs[arr][ph]
 
         def at(p):

time: 174 us -> 172 us (0.989)
  Pallas kernels: 174 us -> 172 us
    pallas_call x1, Pallas kernels: 169 us -> 167 us  [local_fn(): pl.pallas_call(update_kernel, name='update', out_shape=(jax.ShapeDtypeStr...]
where the time goes in v5:
time: 172 us
  Pallas kernels  172 us (100%)
    pallas_call x1, Pallas kernels, local_fn(): pl.pallas_call(update_kernel, name='update', out_shape=(jax.ShapeDtypeStr...  167 us
    pallas_call x1, Pallas kernels, local_fn(): pl.pallas_call(last_kernel, name='last', out_shape=jax.ShapeDtypeStruct((...  5.36 us

profile of v5, /device:TPU:1, one launch (start us, length us, event | category | flops | bytes accessed | tf_op | source)
XLA Modules:
  0.0 172.3 jit_solution(10043597288223258089)
XLA Ops:
  0.0 166.8 %update.1 = (bf16[12,1536,128]{2,1,0:T(8,128)(2,1)}, bf16[2,4,4,4,8,256]{5,4,3,2,1,0:T(8,128)(2,1)}, bf16[2,4,4,4,8,256]{5,4,3,2,1,0:T(8,128)(2,1)}, bf16[12,256,128]{2,1,0:T(8,128)(2,1)}) custom-call(bf16[12,1536,128]{2,1,0:T(8,128)(2,1)} %z_hbm.3, s32[12,1536]{1,0:T(8,128)} %refs_0_.1, bf16[1,128]{1,0:T(2,128)(2,1)} %bitcast.8, bf16[1,128]{1,0:T(2,128)(2,1)} %bitcast.9, ...), custom_call_target="tpu_custom_call" | custom-call | tf_op jit(solution)/shard_map/update/pallas_call | solution.py:423
  166.8 5.4 %last.1 = bf16[12,1536,128]{2,1,0:T(8,128)(2,1)} custom-call(bf16[12,1536,128]{2,1,0:T(8,128)(2,1)} %get-tuple-element.9.part, bf16[2,4,4,4,8,256]{5,4,3,2,1,0:T(8,128)(2,1)} %get-tuple-element.10.own_hbm, bf16[2,4,4,4,8,256]{5,4,3,2,1,0:T(8,128)(2,1)} %get-tuple-element.11.par_hbm, bf16[12,256,128]{2,1,0:T(8,128)(2,1)} %get-tuple-element.12.x_hbm, ...), custom_call_target="tpu_custom_call" | custom-call | tf_op jit(solution)/shard_map/last/pallas_call | solution.py:438

commit v6 on v5

--- a/solution.py
+++ b/solution.py
@@ -146,6 +146,9 @@
     def put(r, v):
         ov[r] = (zv[r].astype(F32) + v).astype(BF)
     hidden_norm(core, lambda i: own_v[:, i // SIDE, i % SIDE].astype(F32), lambda i: par_v[:, i // SIDE, i % SIDE].astype(F32), y, lambda: None)
+    for a, b in zip(ins, outs):
+        a.wait()
+        b.start()
     for cp in loads[4:]:
         cp.wait()
     ends = []
@@ -154,10 +157,6 @@
         out_rows(core, y, hid, wo_ref, wg_ref, lambda r: xv[r], put, n * RL // 2, RL // 2)
         ends.append(pltpu.make_async_copy(ov.at[rows], out_hbm.at[rows, cols, :], osem.at[PASS + n]))
         ends[-1].start()
-        if n == 0:
-            for a, b in zip(ins, outs):
-                a.wait()
-                b.start()
     for cp in outs + ends:
         cp.wait()
 
@@ -195,7 +194,6 @@
     for i, w in enumerate((wa_ref, wag_ref, wb_ref, wbg_ref)):
         wt[i] = w[...].astype(F32).T.astype(BF)
     mall[core] = mask_ref[...]
-    set_hidden(hid, hs_ref, hb_ref)
     scale = scale_ref[...].astype(F32)
     bias = bias_ref[...].astype(F32)
     half = pl.ds(pl.multiple_of(core * CH, CH), CH)
@@ -213,7 +211,7 @@
                 var = jnp.mean(centered * centered, axis=-1, keepdims=True)
                 xall[core * RL + r, at, :] = (centered * lax.rsqrt(var + LN_EPS) * scale + bias).astype(BF)
             return carry
-        lax.fori_loop(0, rows, body, 0, unroll=4 if width == KC else 1)
+        lax.fori_loop(0, rows, body, 0, unroll=8 if width == KC else 1)
 
     def give_x(row0, rows, start, width, sem):
         block = xall.at[pl.ds(core * RL + row0, rows), pl.ds(start, width)]
@@ -266,7 +264,7 @@
                     stage_a[kt, pl.ds(i, CH, stride=SKEW), :] = a[:, lanes]
                     stage_b[kt, pl.ds(i, CH, stride=SKEW), :] = b[:, lanes]
             return carry
-        lax.fori_loop(0, TR, project_row, 0, unroll=4)
+        lax.fori_loop(0, TR, project_row, 0, unroll=8 if width == KC else 4)
         for arr, stage in ((0, stage_b), (1, stage_a)):
             s_ref = bufs[arr][0]
 
@@ -322,6 +320,7 @@
 
     x_copy = pltpu.make_async_copy(xall.at[pl.ds(core * RL, RL), qcols(NQ - 1)], x_out, msem)
     x_copy.start()
+    set_hidden(hid, hs_ref, hb_ref)
 
     def part_sem(s, q, ph):
         k = 2 * NG * NQ + q if ph == 2 else (s * NQ + q) * 2 + ph

time: 172 us -> 172 us (level)
  no operation moved by 1% of the time
where the time goes in v6:
time: 172 us; the launch traced here: 171 us
  Pallas kernels  171 us (99%)
    pallas_call x1, Pallas kernels, local_fn(): pl.pallas_call(update_kernel, name='update', out_shape=(jax.ShapeDtypeStr...  167 us
    pallas_call x1, Pallas kernels, local_fn(): pl.pallas_call(last_kernel, name='last', out_shape=jax.ShapeDtypeStruct((...  4.65 us

profile of v6, /device:TPU:1, one launch (start us, length us, event | category | flops | bytes accessed | tf_op | source)
XLA Modules:
  0.0 171.4 jit_solution(16554263407460077256)
XLA Ops:
  0.0 166.6 %update.1 = (bf16[12,1536,128]{2,1,0:T(8,128)(2,1)}, bf16[2,4,4,4,8,256]{5,4,3,2,1,0:T(8,128)(2,1)}, bf16[2,4,4,4,8,256]{5,4,3,2,1,0:T(8,128)(2,1)}, bf16[12,256,128]{2,1,0:T(8,128)(2,1)}) custom-call(bf16[12,1536,128]{2,1,0:T(8,128)(2,1)} %z_hbm.3, s32[12,1536]{1,0:T(8,128)} %refs_0_.1, bf16[1,128]{1,0:T(2,128)(2,1)} %bitcast.8, bf16[1,128]{1,0:T(2,128)(2,1)} %bitcast.9, ...), custom_call_target="tpu_custom_call" | custom-call | tf_op jit(solution)/shard_map/update/pallas_call | solution.py:422
  166.6 4.7 %last.1 = bf16[12,1536,128]{2,1,0:T(8,128)(2,1)} custom-call(bf16[12,1536,128]{2,1,0:T(8,128)(2,1)} %get-tuple-element.9.part, bf16[2,4,4,4,8,256]{5,4,3,2,1,0:T(8,128)(2,1)} %get-tuple-element.10.own_hbm, bf16[2,4,4,4,8,256]{5,4,3,2,1,0:T(8,128)(2,1)} %get-tuple-element.11.par_hbm, bf16[12,256,128]{2,1,0:T(8,128)(2,1)} %get-tuple-element.12.x_hbm, ...), custom_call_target="tpu_custom_call" | custom-call | tf_op jit(solution)/shard_map/last/pallas_call | solution.py:437

commit v7 on v6

--- a/solution.py
+++ b/solution.py
@@ -425,9 +425,9 @@
             in_specs=[aspec] * 12, out_specs=(aspec,) * 4,
             scratch_shapes=[VMEM((RL, N), jnp.int32), line, line] + [square] * 6 + [line] * 2 + [
                 VMEM((RL, N, C), BF), VMEM((2 * RL, N, C), BF), VMEM((2, RL, N), jnp.int32), VMEM((4, C, C), BF),
-                VMEM((KT // 128, CH * SKEW, 128), F32), VMEM((KT // 128, CH * SKEW, 128), F32),
+                VMEM((KT // 128, CH * SKEW + 16, 128), F32), VMEM((KT // 128, CH * SKEW + 16, 128), F32),
                 sets, sets, sets, sets, sets, sets, sets, VMEM((SIDE, SIDE, SIDE, NG, TR, N), BF),
-                VMEM((KQ // 128, 2 * TR * YSK, 128), F32), VMEM((2, RL, KQ, C), BF), VMEM((2, C, C), F32),
+                VMEM((KQ // 128, (2 * TR + 1) * YSK + 7, 128), F32), VMEM((2, RL, KQ, C), BF), VMEM((2, C, C), F32),
                 DMA((N // PARTS[0][1] + 1,)), DMA, DMA((N // PARTS[0][1],)), DMA, DMA, DMA, DMA((2, 3)), DMA((2, len(UNITS), 2)),
                 DMA((NG + 1,)), DMA, DMA((NQ,)), DMA((NQ,)), pltpu.SemaphoreType.REGULAR, DMA((11,))],
             compiler_params=pltpu.CompilerParams(collective_id=1, has_side_effects=True, vmem_limit_bytes=67043328),
@@ -438,7 +438,7 @@
             last_kernel, name='last', out_shape=jax.ShapeDtypeStruct((RL, N, C), BF),
             in_specs=[aspec] * 9, out_specs=aspec,
             scratch_shapes=[VMEM((RL, N - KQ, C), BF), edge_v, edge_v, block, block, square, square, line, line, block,
-                            VMEM((KQ // 128, 2 * TR * YSK, 128), F32), VMEM((2, C, C), F32), DMA((8,)), DMA((PASS,)), DMA((PASS + 2,))],
+                            VMEM((KQ // 128, (2 * TR + 1) * YSK + 7, 128), F32), VMEM((2, C, C), F32), DMA((8,)), DMA((PASS,)), DMA((PASS + 2,))],
             compiler_params=pltpu.CompilerParams(vmem_limit_bytes=60 * 2**20),
         )(part, own, par, x_last, z_loc, w_gate, w_out, hs, hb)
 

time: 172 us -> 172 us (level)
  no operation moved by 1% of the time
where the time goes in v7:
time: 172 us; the launch traced here: 171 us
  Pallas kernels  171 us (99%)
    pallas_call x1, Pallas kernels, local_fn(): pl.pallas_call(update_kernel, name='update', out_shape=(jax.ShapeDtypeStr...  167 us
    pallas_call x1, Pallas kernels, local_fn(): pl.pallas_call(last_kernel, name='last', out_shape=jax.ShapeDtypeStruct((...  4.65 us

profile of v7, /device:TPU:1, one launch (start us, length us, event | category | flops | bytes accessed | tf_op | source)
XLA Modules:
  0.0 171.4 jit_solution(2682258330930355537)
XLA Ops:
  0.0 166.6 %update.1 = (bf16[12,1536,128]{2,1,0:T(8,128)(2,1)}, bf16[2,4,4,4,8,256]{5,4,3,2,1,0:T(8,128)(2,1)}, bf16[2,4,4,4,8,256]{5,4,3,2,1,0:T(8,128)(2,1)}, bf16[12,256,128]{2,1,0:T(8,128)(2,1)}) custom-call(bf16[12,1536,128]{2,1,0:T(8,128)(2,1)} %z_hbm.3, s32[12,1536]{1,0:T(8,128)} %refs_0_.1, bf16[1,128]{1,0:T(2,128)(2,1)} %bitcast.8, bf16[1,128]{1,0:T(2,128)(2,1)} %bitcast.9, ...), custom_call_target="tpu_custom_call" | custom-call | tf_op jit(solution)/shard_map/update/pallas_call | solution.py:422
  166.6 4.7 %last.1 = bf16[12,1536,128]{2,1,0:T(8,128)(2,1)} custom-call(bf16[12,1536,128]{2,1,0:T(8,128)(2,1)} %get-tuple-element.9.part, bf16[2,4,4,4,8,256]{5,4,3,2,1,0:T(8,128)(2,1)} %get-tuple-element.10.own_hbm, bf16[2,4,4,4,8,256]{5,4,3,2,1,0:T(8,128)(2,1)} %get-tuple-element.11.par_hbm, bf16[12,256,128]{2,1,0:T(8,128)(2,1)} %get-tuple-element.12.x_hbm, ...), custom_call_target="tpu_custom_call" | custom-call | tf_op jit(solution)/shard_map/last/pallas_call | solution.py:437
